TPU v7x, 32 devices: a whole 2x2x4 slice. The times are simulated.
32 devices in a mesh: fsdp: 4 (over z), width: 4 (over y, x), trial: 2 (over core).
Axes of the slice: x: 2, y: 2, z: 4, core: 2. Of those that a mesh axis runs over, the one named last changes fastest.
Arguments:
- weight_query: bfloat16 [7168, 4096], P(('trial', 'fsdp'), 'width'), parts along dimension 0, may hold values from -0.125 to 0.125
- low_query: bfloat16 [7168, 16], P(('trial', 'fsdp')), parts along dimension 0, may hold values from -0.09375 to 0.09375
- high_query: bfloat16 [32, 4096], P('trial', 'width'), parts along dimension 0, may hold values from -1.5 to 1.5
- weight_key: bfloat16 [7168, 2048], P(('trial', 'fsdp'), 'width'), parts along dimension 0, may hold values from -0.125 to 0.125
- low_key: bfloat16 [7168, 16], P(('trial', 'fsdp')), parts along dimension 0, may hold values from -0.09375 to 0.09375
- high_key: bfloat16 [32, 2048], P('trial', 'width'), parts along dimension 0, may hold values from -1.5 to 1.5
- weight_value: bfloat16 [7168, 2048], P(('trial', 'fsdp'), 'width'), parts along dimension 0, may hold values from -0.125 to 0.125
- low_value: bfloat16 [7168, 16], P(('trial', 'fsdp')), parts along dimension 0, may hold values from -0.09375 to 0.09375
- high_value: bfloat16 [32, 2048], P('trial', 'width'), parts along dimension 0, may hold values from -1.5 to 1.5
- norm_train: float32 [7168], P(('trial', 'fsdp', 'width')), parts along dimension 0, may hold values from 0.25 to 1.75
- norm_step: float32 [7168], P(('trial', 'fsdp', 'width')), parts along dimension 0, may hold values from -0.3 to 0.3
Outputs:
- final_query: bfloat16 [7168, 4096], P('trial', 'width'), parts along dimension 0
- final_key: bfloat16 [7168, 2048], P('trial', 'width'), parts along dimension 0
- final_value: bfloat16 [7168, 2048], P('trial', 'width'), parts along dimension 0
- column_query: float32 [8192], P(('trial', 'width')), parts along dimension 0
- column_key: float32 [4096], P(('trial', 'width')), parts along dimension 0
- column_value: float32 [4096], P(('trial', 'width')), parts along dimension 0
- serve_norm: bfloat16 [7168], P('trial'), parts along dimension 0
There are 2 independent parts, one for each index of `trial`. A program takes and returns all parts, laid end to end along the dimension named above; each array names one. Nothing has to cross between parts.
All inputs are finite; a program needn't handle non-finite values. Where the computation divides by a largest or mean magnitude, that divisor is 1e-20 or more.
Results may differ from a plain program's by a relative error of at most 0.001.
Values may be sent and summed in bfloat16 or wider, within the bound.
A program may use at most 64 MiB of HBM per device.

v0:
```python
import functools

import jax
import jax.numpy as jnp
from jax import lax
from jax.experimental import pallas as pl
from jax.experimental.pallas import tpu as pltpu
from jax.sharding import PartitionSpec as P

mix_rate = 2.0
MESH = pl.DeviceIdType.MESH
F32, BF16 = jnp.float32, jnp.bfloat16


def pieces_of(rows, widths):
    smallest = min(widths)
    pieces = []
    for a, width in enumerate(widths):
        count = 2 * (width // smallest)
        while rows % (count * 8):
            count //= 2
        pieces += [(a, i * (rows // count), rows // count) for i in range(count)]
    return pieces


def gather_kernel(n, m, wq, wk, wv, lq, lk, lv, hq, hk, hv, nt, ns,
                  gq, gk, gv, tail, glow, col_out, norm_out,
                  low_q, low_k, low_v, high_q, high_k, high_v, train, step_v, col_ref, norm_ref,
                  small_sem, result_sem,
                  own_q, own_k, own_v, mx, mx_own, nrm, nrm_own,
                  send_up, send_dn, recv_up, recv_dn,
                  low_send, low_recv, peer_send, peer_recv,
                  in_sem, out_sem, low_sem, mx_send, mx_recv, nrm_send, nrm_recv):
    z, x = lax.axis_index("fsdp"), lax.axis_index("width")
    weights, gathered, owns = (wq, wk, wv), (gq, gk, gv), (own_q, own_k, own_v)
    lows, near_lows, near_highs = (lq, lk, lv), (low_q, low_k, low_v), (high_q, high_k, high_v)
    rows = wq.shape[0]
    rank = hq.shape[0]
    pieces = pieces_of(rows, [w.shape[1] for w in weights])
    count = len(pieces)
    ways = (True, False)

    barrier = pltpu.get_barrier_semaphore()
    for dz in range(n):
        for dx in range(m):
            if dz or dx:
                pl.semaphore_signal(
                    barrier, inc=1, device_id_type=MESH,
                    device_id={"fsdp": lax.rem(z + dz, n), "width": lax.rem(x + dx, m)},
                )
    pl.semaphore_wait(barrier, n * m - 1)

    def sent_block(hop, up):
        return jnp.clip(z - (hop - 1) if up else z + (hop - 1), 0, n - 1)

    def next_on(up):
        return jnp.clip(z + 1 if up else z - 1, 0, n - 1)

    def piece(hop, c, up, aside=False):
        a, first, size = pieces[c]
        block = sent_block(hop, up)
        landing = gathered[a].at[block, pl.ds(first, size)]
        source = weights[a].at[pl.ds(first, size)] if hop == 1 else landing
        if aside:
            landing = tail.at[pl.ds(first, size)]
        out, back = (send_up, recv_up) if up else (send_dn, recv_dn)
        return pltpu.make_async_remote_copy(
            src_ref=source, dst_ref=landing,
            send_sem=out.at[hop - 1, c], recv_sem=back.at[hop - 1, c],
            device_id={"fsdp": next_on(up)}, device_id_type=MESH,
        )

    def start_piece(hop, c, up):
        if hop == n - 2 and pieces[c][0] == 2:
            aside = (z == n - 3) if up else (z == 2)

            @pl.when(sends(hop, up) & aside)
            def _():
                piece(hop, c, up, True).start()

            @pl.when(sends(hop, up) & jnp.logical_not(aside))
            def _():
                piece(hop, c, up).start()
        else:
            @pl.when(sends(hop, up))
            def _():
                piece(hop, c, up).start()

    def travels(hop, c):
        return not (hop == n - 1 and pieces[c][0] == 2)

    def sends(hop, up):
        return (z >= hop - 1) & (z < n - 1) if up else (z + hop - 1 <= n - 1) & (z > 0)

    def receives(hop, up):
        return z >= hop if up else z + hop <= n - 1

    def low_slot(block, i):
        return glow.at[block, pl.ds(i * rank, rank)]

    def low_piece(hop, i, up):
        block = sent_block(hop, up)
        return pltpu.make_async_remote_copy(
            src_ref=lows[i] if hop == 1 else low_slot(block, i), dst_ref=low_slot(block, i),
            send_sem=low_send.at[int(up), hop - 1, i], recv_sem=low_recv.at[int(up), hop - 1, i],
            device_id={"fsdp": next_on(up)}, device_id_type=MESH)

    def low_peer(hop, i, up, dx):
        block = jnp.clip(z - hop if up else z + hop, 0, n - 1)
        return pltpu.make_async_remote_copy(
            src_ref=low_slot(block, i), dst_ref=low_slot(block, i),
            send_sem=peer_send.at[int(up), hop - 1, i * (m - 1) + dx - 1],
            recv_sem=peer_recv.at[int(up), hop - 1, i],
            device_id={"width": lax.rem(x + dx, m)}, device_id_type=MESH)

    for i in range(3):
        for up in ways:
            @pl.when((x == i % m) & sends(1, up))
            def _(i=i, up=up):
                low_piece(1, i, up).start()
    for c in range(count):
        for up in ways:
            start_piece(1, c, up)
    loads = [pltpu.make_async_copy(w, o, in_sem.at[i]) for i, (w, o) in enumerate(zip(weights, owns))]
    for load in loads:
        load.start()
    smalls = [
        pltpu.make_async_copy(a, b, small_sem.at[i])
        for i, (a, b) in enumerate(zip(lows + (hq, hk, hv, nt, ns), near_lows + near_highs + (train, step_v)))
    ]
    for small in smalls:
        small.start()
    for small in smalls:
        small.wait()
    places = [pltpu.make_async_copy(low, low_slot(z, i), low_sem.at[i]) for i, low in enumerate(near_lows)]
    for place in places:
        place.start()
    nrm_own[...] = train[...] + step_v[...]

    for load in loads:
        load.wait()
    stores = [pltpu.make_async_copy(o, g.at[z], out_sem.at[i]) for i, (g, o) in enumerate(zip(gathered, owns))]
    for store in stores:
        store.start()
    tile = 128 if rows % 128 == 0 else rows
    at = 0
    for low, high, own in zip(near_lows, near_highs, owns):
        width = own.shape[1]

        def step(i, best, low=low, high=high, own=own):
            span = pl.ds(pl.multiple_of(i * tile, tile), tile)
            delta = lax.dot_general(
                low[:, span], high[...], (((0,), (0,)), ((), ())), preferred_element_type=F32)
            result = own[span, :].astype(F32) + mix_rate * delta
            return jnp.maximum(best, jnp.max(jnp.abs(result), axis=0, keepdims=True))

        mx_own[:, pl.ds(at, width)] = lax.fori_loop(0, rows // tile, step, jnp.zeros((1, width), F32))
        at += width

    def maxima(d):
        return pltpu.make_async_remote_copy(
            src_ref=mx_own, dst_ref=mx.at[d - 1], send_sem=mx_send.at[d - 1], recv_sem=mx_recv.at[d - 1],
            device_id={"fsdp": lax.rem(z + d, n)}, device_id_type=MESH)

    def gains(dz, dx):
        d = dz * m + dx
        return pltpu.make_async_remote_copy(
            src_ref=nrm_own, dst_ref=nrm.at[d - 1], send_sem=nrm_send.at[d - 1], recv_sem=nrm_recv.at[d - 1],
            device_id={"fsdp": lax.rem(z + dz, n), "width": lax.rem(x + dx, m)}, device_id_type=MESH)

    for d in range(1, n):
        maxima(d).start()
    for d in range(1, n * m):
        gains(d // m, d % m).start()

    for hop in range(1, n):
        for i in range(3):
            for up in ways:
                @pl.when((x == i % m) & receives(hop, up))
                def _(hop=hop, i=i, up=up):
                    low_piece(hop, i, up).wait_recv()
                    if hop < n - 1:
                        @pl.when(sends(hop + 1, up))
                        def _():
                            low_piece(hop + 1, i, up).start()
                    for dx in range(1, m):
                        low_peer(hop, i, up, dx).start()
        for c in range(count):
            if not travels(hop, c):
                continue
            for up in ways:
                @pl.when(receives(hop, up))
                def _(hop=hop, c=c, up=up):
                    piece(hop, c, up).wait_recv()
                if hop < n - 1 and travels(hop + 1, c):
                    start_piece(hop + 1, c, up)
        if hop == 1:
            best = mx_own[...]
            for d in range(1, n):
                maxima(d).wait_recv()
                best = jnp.maximum(best, mx[d - 1])
            col_ref[...] = best
            norm_ref[z * m + x] = nrm_own[...]
            for d in range(1, n * m):
                gains(d // m, d % m).wait_recv()
                norm_ref[lax.rem(z + n - d // m, n) * m + lax.rem(x + m - d % m, m)] = nrm[d - 1]
            results = [pltpu.make_async_copy(col_ref, col_out, result_sem.at[0]),
                       pltpu.make_async_copy(norm_ref, norm_out, result_sem.at[1])]
            for result in results:
                result.start()
    for copy in stores + places + results:
        copy.wait()
    for d in range(1, n):
        maxima(d).wait_send()
    for d in range(1, n * m):
        gains(d // m, d % m).wait_send()
    for hop in range(1, n):
        for up in ways:
            for i in range(3):
                @pl.when((x == i % m) & sends(hop, up))
                def _(hop=hop, up=up, i=i):
                    low_piece(hop, i, up).wait_send()

                @pl.when((x == i % m) & receives(hop, up))
                def _(hop=hop, up=up, i=i):
                    for dx in range(1, m):
                        low_peer(hop, i, up, dx).wait_send()

                @pl.when((x != i % m) & receives(hop, up))
                def _(hop=hop, up=up, i=i):
                    low_peer(hop, i, up, 1).wait_recv()

            @pl.when(sends(hop, up))
            def _(hop=hop, up=up):
                for c in range(count):
                    if travels(hop, c):
                        piece(hop, c, up).wait_send()


def merged(weight, low, high, scale):
    delta = lax.dot_general(low, high, (((0,), (0,)), ((), ())), preferred_element_type=F32)
    return ((weight.astype(F32) + mix_rate * delta) * scale).astype(BF16)


def merge_kernel(tile, gq, gk, gv, glow, hq, hk, hv, col_q, col_k, col_v, fq, fk, fv, cq, ck, cv):
    rank = hq.shape[0]
    arrays = ((gq, hq, col_q, fq), (gk, hk, col_k, fk), (gv, hv, col_v, fv))
    for col, c in ((col_q, cq), (col_k, ck), (col_v, cv)):
        c[...] = col[...]

    def step(t, carry):
        span = pl.ds(pl.multiple_of(t * tile, tile), tile)
        for i, (g, high, col, f) in enumerate(arrays):
            low = glow[0, pl.ds(i * rank, rank), span]
            f[span, :] = merged(g[0, span, :], low, high[...], 1.0 / col[...])
        return carry

    lax.fori_loop(0, gq.shape[1] // tile, step, 0)


def last_kernel(n, parts, came, tail, glow, high, col, before, final, out_ref, out_sem):
    z = lax.axis_index("fsdp")
    rank, width = high.shape
    rows = came.shape[0]
    size = rows // parts
    outer = (z == 0) | (z == n - 1)
    block = jnp.where(z < 2, n - 1, 0)

    def store(p):
        return pltpu.make_async_copy(
            out_ref.at[pl.ds(p * size, size)],
            final.at[pl.ds(pl.multiple_of(block * rows + p * size, 8), size)], out_sem.at[p])

    def write(source):
        scale = 1.0 / col[:, pl.ds(col.shape[1] - width, width)]
        for p in range(parts):
            span = pl.ds(p * size, size)
            low = glow[block, pl.ds(2 * rank, rank), span]
            out_ref[span, :] = merged(source[span, :], low, high[...], scale)
            store(p).start()
        for p in range(parts):
            store(p).wait()

    @pl.when(outer)
    def _():
        write(came)

    @pl.when((z == 1) | (z == n - 2))
    def _():
        write(tail)


def local(n, m, wq, lq, hq, wk, lk, hk, wv, lv, hv, nt, ns):
    rows, cq = wq.shape
    ck, cv = wk.shape[1], wv.shape[1]
    rank, share = hq.shape[0], nt.shape[0]
    total = cq + ck + cv
    count = len(pieces_of(rows, [cq, ck, cv]))
    hbm, vmem = pl.BlockSpec(memory_space=pl.ANY), pl.BlockSpec(memory_space=pltpu.VMEM)
    dma = pltpu.SemaphoreType.DMA
    gq, gk, gv, tail, glow, col, norm = pl.pallas_call(
        functools.partial(gather_kernel, n, m),
        out_shape=[
            jax.ShapeDtypeStruct((n, rows, cq), BF16),
            jax.ShapeDtypeStruct((n, rows, ck), BF16),
            jax.ShapeDtypeStruct((n, rows, cv), BF16),
            jax.ShapeDtypeStruct((rows, cv), BF16),
            jax.ShapeDtypeStruct((n, 3 * rank, rows), BF16),
            jax.ShapeDtypeStruct((1, total), F32),
            jax.ShapeDtypeStruct((n * m, 1, share), F32),
        ],
        in_specs=[hbm] * 11,
        out_specs=[hbm] * 7,
        scratch_shapes=[
            pltpu.VMEM((rank, rows), BF16), pltpu.VMEM((rank, rows), BF16), pltpu.VMEM((rank, rows), BF16),
            pltpu.VMEM((rank, cq), BF16), pltpu.VMEM((rank, ck), BF16), pltpu.VMEM((rank, cv), BF16),
            pltpu.VMEM((1, share), F32), pltpu.VMEM((1, share), F32),
            pltpu.VMEM((1, total), F32), pltpu.VMEM((n * m, 1, share), F32), dma((8,)), dma((2,)),
            pltpu.VMEM((rows, cq), BF16), pltpu.VMEM((rows, ck), BF16), pltpu.VMEM((rows, cv), BF16),
            pltpu.VMEM((n - 1, 1, total), F32), pltpu.VMEM((1, total), F32),
            pltpu.VMEM((n * m - 1, 1, share), F32), pltpu.VMEM((1, share), F32),
            dma((n - 1, count)), dma((n - 1, count)), dma((n - 1, count)), dma((n - 1, count)),
            dma((2, n - 1, 3)), dma((2, n - 1, 3)), dma((2, n - 1, 3 * (m - 1))), dma((2, n - 1, 3)),
            dma((3,)), dma((3,)), dma((3,)), dma((n - 1,)), dma((n - 1,)), dma((n * m - 1,)), dma((n * m - 1,)),
        ],
        compiler_params=pltpu.CompilerParams(collective_id=0, has_side_effects=True),
    )(wq, wk, wv, lq.T, lk.T, lv.T, hq, hk, hv, nt.reshape(1, share), ns.reshape(1, share))

    came = lax.ppermute(tail, "fsdp", [(1, 0), (n - 2, n - 1)])

    tile = 128 if rows % 128 == 0 else rows
    halves = 2 if min(cq, ck, cv) % 256 == 0 and ck == cv and cq % ck == 0 else 1
    starts = (0, cq, cq + ck)
    widths = (cq // halves, ck // halves, cv // halves)

    def block(width):
        return pl.BlockSpec((1, rows, width), lambda j, i: (i, 0, j))

    def placed(width):
        return pl.BlockSpec((rows, width), lambda j, i: (i, j))

    def columns(height, width):
        return pl.BlockSpec((height, width), lambda j, i: (0, j))

    def scales(start, width):
        return pl.BlockSpec((1, width), lambda j, i: (0, start // width + j))

    fq, fk, before, col_q, col_k, col_v = pl.pallas_call(
        functools.partial(merge_kernel, tile),
        grid=(halves, n),
        out_shape=[jax.ShapeDtypeStruct((n * rows, c), BF16) for c in (cq, ck, cv)]
        + [jax.ShapeDtypeStruct((1, c), F32) for c in (cq, ck, cv)],
        in_specs=[block(c) for c in widths]
        + [pl.BlockSpec((1, 3 * rank, rows), lambda j, i: (i, 0, 0))]
        + [columns(rank, c) for c in widths]
        + [scales(start, c) for start, c in zip(starts, widths)],
        out_specs=[placed(c) for c in widths] + [columns(1, c) for c in widths],
        cost_estimate=pl.CostEstimate(
            flops=2 * n * rows * total * rank, bytes_accessed=4 * n * rows * total, transcendentals=0),
    )(gq, gk, gv, glow, hq, hk, hv, col, col, col)

    parts = 7 if rows % (7 * 128) == 0 else 1
    fv = pl.pallas_call(
        functools.partial(last_kernel, n, parts),
        out_shape=jax.ShapeDtypeStruct((n * rows, cv), BF16),
        in_specs=[vmem] * 5 + [hbm],
        out_specs=hbm,
        scratch_shapes=[
            pltpu.VMEM((rows, cv), BF16), dma((parts,)),
        ],
        input_output_aliases={5: 0},
        cost_estimate=pl.CostEstimate(
            flops=2 * rows * cv * rank, bytes_accessed=4 * rows * cv, transcendentals=0),
    )(came, tail, glow, hv, col, before)
    return (fq, fk, fv, col_q[0], col_k[0], col_v[0], norm.reshape(-1).astype(BF16))


def solution(mesh):
    placed = (
        P(("trial", "fsdp"), "width"), P(("trial", "fsdp"), None), P("trial", "width"),
        P(("trial", "fsdp"), "width"), P(("trial", "fsdp"), None), P("trial", "width"),
        P(("trial", "fsdp"), "width"), P(("trial", "fsdp"), None), P("trial", "width"),
        P(("trial", "fsdp", "width")), P(("trial", "fsdp", "width")),
    )
    return jax.shard_map(
        functools.partial(local, mesh.shape["fsdp"], mesh.shape["width"]),
        mesh=mesh,
        in_specs=placed,
        out_specs=(
            P("trial", "width"), P("trial", "width"), P("trial", "width"),
            P(("trial", "width")), P(("trial", "width")), P(("trial", "width")),
            P("trial"),
        ),
        check_vma=False,
    )
```

profile of v0, /device:TPU:4, one launch (start us, length us, event | category | flops | bytes accessed | tf_op | source)
XLA Modules:
  0.0 255.1 jit_solution(7146890837329702513)
XLA Ops:
  0.6 227.4 %shard_map.162 = (bf16[4,896,1024]{2,1,0:T(8,128)(2,1)}, bf16[4,896,512]{2,1,0:T(8,128)(2,1)}, bf16[4,896,512]{2,1,0:T(8,128)(2,1)}, bf16[896,512]{1,0:T(8,128)(...) custom-call(bf16[896,1024]{1,0:T(8,128)(2,1)} %wq.1, bf16[896,512]{1,0:T(8,128)(2,1)} %wk.1, ...), custom_call_target="tpu_custom_call" | custom-call | tf_op jit(solution)/shard_map/pallas_call | solution.py:301
  228.1 1.3 collective-permute-start
  229.4 0.8 convert_reduce_fusion
  230.1 0.7 convert_element_type.7
  230.8 18.6 %shard_map.163 = (bf16[3584,1024]{1,0:T(8,128)(2,1)}, bf16[3584,512]{1,0:T(8,128)(2,1)}, bf16[3584,512]{1,0:T(8,128)(2,1)}, f32[1,1024]{1,0:T(1,128)}, f32[1,512]{1,0:T(1,128)}, /*index=5*/f32[1,512]{1,0:T(1,128)}) custom-call(bf16[4,896,1024]{2,1,0:T(8,128)(2,1)} %get-tuple-element.20.gq, bf16[4,896,512]{2,1,0:T(8,128)(2,1)} %get-tuple-element.21.gk, ...), custom_call_target="tpu_custom_call" | custom-call | flops 234881024 | bytes 29360128 | tf_op jit(solution)/shard_map/pallas_call | solution.py:348
  249.4 2.0 collective-permute-done.came
  251.4 0.0 copy-start
  251.4 0.9 copy-done
  252.3 2.7 %shard_map.164 = bf16[3584,512]{1,0:T(8,128)(2,1)} custom-call(bf16[896,512]{1,0:T(8,128)(2,1)} %copy-done, bf16[896,512]{1,0:T(8,128)(2,1)} %get-tuple-element.27.tail, bf16[4,48,896]{2,1,0:T(8,128)(2,1)} %get-tuple-element.23.glow, bf16[16,512]{1,0:T(8,128)(2,1)} %high.1, ...), custom_call_target="tpu_custom_call", output_to_operand_aliasing={{}: (5, {})} | custom-call | flops 14680064 | bytes 1835008 | tf_op jit(solution)/shard_map/pallas_call | solution.py:363
Async XLA Ops:
  228.1 23.3 %collective-permute-start = (bf16[896,512]{1,0:T(8,128)(2,1)}, bf16[896,512]{1,0:T(8,128)(2,1)S(1)}, u32[]{:S(2)}, u32[]{:S(2)}) collective-permute-start(bf16[896,512]{1,0:T(8,128)(2,1)} %get-tuple-element.27.tail), channel_id=1, source_target_pairs={{8,0},{16,24},{9,1},{17,25},{10,2},{18,26},{11,3},{19,27},{12,4},{... | collective-permute-start | bytes 2752520 | tf_op jit(solution)/shard_map/ppermute | solution.py:329
  251.4 0.9 copy-start
where the time goes:
time: 258 us; the launch traced here: 255 us
  Pallas kernels  249 us (97%)
    pallas_call x1, Pallas kernels, local(): pl.pallas_call(functools.partial(gather_kernel, n, m), out_shape=[jax.Sha...  227 us
    pallas_call x1, Pallas kernels, local(): pl.pallas_call(functools.partial(merge_kernel, tile), grid=(halves, n), o...  18.6 us
  transfers between devices with their start and end apart: 1, of which 1 were waited for; matrix products, arithmetic and copies ran while one was open for 1% of the time, Pallas kernels for 7%

commit v1 on v0

v1 whole, which is shorter than its diff:
```python
import functools

import jax
import jax.numpy as jnp
from jax import lax
from jax.experimental import pallas as pl
from jax.experimental.pallas import tpu as pltpu
from jax.sharding import PartitionSpec as P

mix_rate = 2.0
MESH = pl.DeviceIdType.MESH
F32, BF16 = jnp.float32, jnp.bfloat16
WAYS = (True, False)


def pieces_of(rows, widths):
    smallest = min(widths)
    pieces = []
    for a, width in enumerate(widths):
        count = 2 * (width // smallest)
        while rows % (count * 8):
            count //= 2
        pieces += [(a, i * (rows // count), rows // count) for i in range(count)]
    return pieces


def carrier(i, m):
    return (m - 1 - i) % m


def line_kernel(n, m, wq, wk, wv, lq, lk, lv, hq, hk, hv, nt, ns,
                gq, gk, gv, tail_k, tail_v, glow, col_out, norm_out,
                low_q, low_k, low_v, high_q, high_k, high_v, train, step_v, col_ref, norm_ref,
                small_sem, result_sem,
                own_q, own_k, own_v, vec, vec_own,
                send_up, send_dn, recv_up, recv_dn,
                low_send, low_recv, vec_send, vec_recv,
                in_sem, out_sem, low_sem):
    z, x = lax.axis_index("fsdp"), lax.axis_index("width")
    weights, gathered, owns = (wq, wk, wv), (gq, gk, gv), (own_q, own_k, own_v)
    asides = {1: tail_k, 2: tail_v}
    lows, near_lows, near_highs = (lq, lk, lv), (low_q, low_k, low_v), (high_q, high_k, high_v)
    rows = wq.shape[0]
    share = train.shape[1]
    pieces = pieces_of(rows, [w.shape[1] for w in weights])
    count = len(pieces)

    loads = [pltpu.make_async_copy(w, o, in_sem.at[i]) for i, (w, o) in enumerate(zip(weights, owns))]
    smalls = [
        pltpu.make_async_copy(a, b, small_sem.at[i])
        for i, (a, b) in enumerate(zip(lows + (hq, hk, hv, nt, ns), near_lows + near_highs + (train, step_v)))
    ]

    barrier = pltpu.get_barrier_semaphore()
    ends = (z == 0) | (z == n - 1)

    @pl.when(z > 0)
    def _():
        pl.semaphore_signal(barrier, inc=1, device_id_type=MESH, device_id={"fsdp": jnp.maximum(z - 1, 0)})

    @pl.when(z < n - 1)
    def _():
        pl.semaphore_signal(barrier, inc=1, device_id_type=MESH, device_id={"fsdp": jnp.minimum(z + 1, n - 1)})

    for copy in loads + smalls:
        copy.start()

    @pl.when(ends)
    def _():
        pl.semaphore_wait(barrier, 1)

    @pl.when(jnp.logical_not(ends))
    def _():
        pl.semaphore_wait(barrier, 2)

    def sent_block(hop, up):
        return jnp.clip(z - (hop - 1) if up else z + (hop - 1), 0, n - 1)

    def came_block(hop, up):
        return jnp.clip(z - hop if up else z + hop, 0, n - 1)

    def next_on(up):
        return jnp.clip(z + 1 if up else z - 1, 0, n - 1)

    def sends(hop, up):
        return (z >= hop - 1) & (z < n - 1) if up else (z + hop - 1 <= n - 1) & (z > 0)

    def receives(hop, up):
        return z >= hop if up else z + hop <= n - 1

    def travels(hop, c):
        return not (hop == n - 1 and pieces[c][0] in asides)

    def piece(hop, c, up, aside=False):
        a, first, size = pieces[c]
        block = sent_block(hop, up)
        landing = gathered[a].at[block, pl.ds(first, size)]
        source = weights[a].at[pl.ds(first, size)] if hop == 1 else landing
        if aside:
            landing = asides[a].at[pl.ds(first, size)]
        out, back = (send_up, recv_up) if up else (send_dn, recv_dn)
        return pltpu.make_async_remote_copy(
            src_ref=source, dst_ref=landing,
            send_sem=out.at[hop - 1, c], recv_sem=back.at[hop - 1, c],
            device_id={"fsdp": next_on(up)}, device_id_type=MESH,
        )

    def start_piece(hop, c, up):
        if hop == n - 2 and pieces[c][0] in asides:
            aside = (z == n - 3) if up else (z == 2)

            @pl.when(sends(hop, up) & aside)
            def _():
                piece(hop, c, up, True).start()

            @pl.when(sends(hop, up) & jnp.logical_not(aside))
            def _():
                piece(hop, c, up).start()
        else:
            @pl.when(sends(hop, up))
            def _():
                piece(hop, c, up).start()

    def low_piece(hop, i, up):
        block = sent_block(hop, up)
        return pltpu.make_async_remote_copy(
            src_ref=lows[i] if hop == 1 else glow.at[block], dst_ref=glow.at[block],
            send_sem=low_send.at[int(up), hop - 1], recv_sem=low_recv.at[int(up), hop - 1],
            device_id={"fsdp": next_on(up)}, device_id_type=MESH)

    def vec_piece(hop, up):
        block = sent_block(hop, up)
        return pltpu.make_async_remote_copy(
            src_ref=vec_own if hop == 1 else vec.at[block], dst_ref=vec.at[block],
            send_sem=vec_send.at[int(up), hop - 1], recv_sem=vec_recv.at[int(up), hop - 1],
            device_id={"fsdp": next_on(up)}, device_id_type=MESH)

    def carried(i):
        return x == carrier(i, m)

    for c in range(count):
        for up in WAYS:
            start_piece(1, c, up)
    for i in range(3):
        for up in WAYS:
            @pl.when(carried(i) & sends(1, up))
            def _(i=i, up=up):
                low_piece(1, i, up).start()

    for small in smalls:
        small.wait()
    for i in range(3):
        @pl.when(carried(i))
        def _(i=i):
            pltpu.make_async_copy(near_lows[i], glow.at[z], low_sem).start()
    for load in loads:
        load.wait()
    stores = [pltpu.make_async_copy(o, g.at[z], out_sem.at[i]) for i, (g, o) in enumerate(zip(gathered, owns))]
    for store in stores:
        store.start()
    total = col_ref.shape[1]
    tile = 128 if rows % 128 == 0 else rows
    at = 0
    for low, high, own in zip(near_lows, near_highs, owns):
        width = own.shape[1]

        def step(i, best, low=low, high=high, own=own):
            span = pl.ds(pl.multiple_of(i * tile, tile), tile)
            delta = lax.dot_general(
                low[:, span], high[...], (((0,), (0,)), ((), ())), preferred_element_type=F32)
            result = own[span, :].astype(F32) + mix_rate * delta
            return jnp.maximum(best, jnp.max(jnp.abs(result), axis=0, keepdims=True))

        vec_own[:, pl.ds(at, width)] = lax.fori_loop(0, rows // tile, step, jnp.zeros((1, width), F32))
        at += width
    gain = train[...] + step_v[...]
    vec_own[:, pl.ds(total, share)] = gain
    norm_ref[z] = gain
    col_ref[...] = vec_own[:, pl.ds(0, total)]

    for up in WAYS:
        @pl.when(sends(1, up))
        def _(up=up):
            vec_piece(1, up).start()

    results = [pltpu.make_async_copy(col_ref, col_out, result_sem.at[0]),
               pltpu.make_async_copy(norm_ref, norm_out, result_sem.at[1])]
    for hop in range(1, n):
        for up in WAYS:
            @pl.when(receives(hop, up))
            def _(hop=hop, up=up):
                for i in range(3):
                    @pl.when(carried(i))
                    def _(i=i):
                        low_piece(hop, i, up).wait_recv()
                        if hop < n - 1:
                            @pl.when(sends(hop + 1, up))
                            def _():
                                low_piece(hop + 1, i, up).start()
        for c in range(count):
            if not travels(hop, c):
                continue
            for up in WAYS:
                @pl.when(receives(hop, up))
                def _(hop=hop, c=c, up=up):
                    piece(hop, c, up).wait_recv()
                if hop < n - 1 and travels(hop + 1, c):
                    start_piece(hop + 1, c, up)
            if c == 1:
                for up in WAYS:
                    @pl.when(receives(hop, up))
                    def _(hop=hop, up=up):
                        vec_piece(hop, up).wait_recv()
                        if hop < n - 1:
                            @pl.when(sends(hop + 1, up))
                            def _():
                                vec_piece(hop + 1, up).start()
                        block = came_block(hop, up)
                        came = vec[block]
                        col_ref[...] = jnp.maximum(col_ref[...], came[:, :total])
                        norm_ref[block] = came[:, total:total + share]
                if hop == n - 1:
                    for result in results:
                        result.start()
    for copy in stores + results:
        copy.wait()
    for i in range(3):
        @pl.when(carried(i))
        def _(i=i):
            pltpu.make_async_copy(near_lows[i], glow.at[z], low_sem).wait()
    for hop in range(1, n):
        for up in WAYS:
            @pl.when(sends(hop, up))
            def _(hop=hop, up=up):
                vec_piece(hop, up).wait_send()
                for i in range(3):
                    @pl.when(carried(i))
                    def _(i=i):
                        low_piece(hop, i, up).wait_send()
                for c in range(count):
                    if travels(hop, c):
                        piece(hop, c, up).wait_send()


def plane_kernel(m, low_ref, norm_ref, glow, norm, low_send, low_recv, norm_send, norm_recv, own_sem):
    x = lax.axis_index("width")
    barrier = pltpu.get_barrier_semaphore()
    for d in range(1, m):
        pl.semaphore_signal(barrier, inc=1, device_id_type=MESH, device_id={"width": lax.rem(x + d, m)})
    own = pltpu.make_async_copy(norm_ref, norm.at[:, x], own_sem.at[1])
    own.start()
    pl.semaphore_wait(barrier, m - 1)

    def low_to(i, d):
        return pltpu.make_async_remote_copy(
            src_ref=low_ref, dst_ref=glow.at[i], send_sem=low_send.at[i, d - 1], recv_sem=low_recv.at[i],
            device_id={"width": lax.rem(x + d, m)}, device_id_type=MESH)

    def norm_to(d):
        return pltpu.make_async_remote_copy(
            src_ref=norm_ref, dst_ref=norm.at[:, x], send_sem=norm_send.at[d - 1], recv_sem=norm_recv.at[d - 1],
            device_id={"width": lax.rem(x + d, m)}, device_id_type=MESH)

    for i in range(3):
        @pl.when(x == carrier(i, m))
        def _(i=i):
            for d in range(1, m):
                low_to(i, d).start()
            pltpu.make_async_copy(low_ref, glow.at[i], own_sem.at[0]).start()
    for d in range(1, m):
        norm_to(d).start()
    own.wait()
    for d in range(1, m):
        norm_to(d).wait()
    for i in range(3):
        @pl.when(x == carrier(i, m))
        def _(i=i):
            pltpu.make_async_copy(low_ref, glow.at[i], own_sem.at[0]).wait()
            for d in range(1, m):
                low_to(i, d).wait_send()

        @pl.when(x != carrier(i, m))
        def _(i=i):
            low_to(i, 1).wait_recv()


def merged(weight, low, high, scale):
    delta = lax.dot_general(low, high, (((0,), (0,)), ((), ())), preferred_element_type=F32)
    return ((weight.astype(F32) + mix_rate * delta) * scale).astype(BF16)


def merge_kernel(tile, gq, gk, gv, glow, hq, hk, hv, col_q, col_k, col_v, fq, fk, fv, cq, ck, cv):
    arrays = ((gq, hq, col_q, fq), (gk, hk, col_k, fk), (gv, hv, col_v, fv))
    for col, c in ((col_q, cq), (col_k, ck), (col_v, cv)):
        c[...] = col[...]

    def step(t, carry):
        span = pl.ds(pl.multiple_of(t * tile, tile), tile)
        for i, (g, high, col, f) in enumerate(arrays):
            f[span, :] = merged(g[0, span, :], glow[i, 0, :, span], high[...], 1.0 / col[...])
        return carry

    lax.fori_loop(0, gq.shape[1] // tile, step, 0)


def last_kernel(n, parts, came, tail, low_first, low_last, high, col, before, final, out_ref, out_sem):
    z = lax.axis_index("fsdp")
    rows = came.shape[0]
    size = rows // parts

    def store(p, block):
        return pltpu.make_async_copy(
            out_ref.at[pl.ds(p * size, size)],
            final.at[pl.ds(block * rows + p * size, size)], out_sem.at[p])

    def write(source, low, block):
        scale = 1.0 / col[...]
        for p in range(parts):
            span = pl.ds(p * size, size)
            out_ref[span, :] = merged(source[span, :], low[0, 0, :, span], high[...], scale)
            store(p, block).start()
        for p in range(parts):
            store(p, block).wait()

    for at, source, low, block in ((0, came, low_last, n - 1), (1, tail, low_last, n - 1),
                                   (n - 2, tail, low_first, 0), (n - 1, came, low_first, 0)):
        @pl.when(z == at)
        def _(source=source, low=low, block=block):
            write(source, low, block)


def local(n, m, wq, lq, hq, wk, lk, hk, wv, lv, hv, nt, ns):
    rows, cq = wq.shape
    ck, cv = wk.shape[1], wv.shape[1]
    rank, share = hq.shape[0], nt.shape[0]
    total = cq + ck + cv
    length = total + -(-share // 128) * 128
    count = len(pieces_of(rows, [cq, ck, cv]))
    hbm, vmem = pl.BlockSpec(memory_space=pl.ANY), pl.BlockSpec(memory_space=pltpu.VMEM)
    dma = pltpu.SemaphoreType.DMA
    gq, gk, gv, tail_k, tail_v, part, col, normz = pl.pallas_call(
        functools.partial(line_kernel, n, m),
        out_shape=[
            jax.ShapeDtypeStruct((n, rows, cq), BF16),
            jax.ShapeDtypeStruct((n, rows, ck), BF16),
            jax.ShapeDtypeStruct((n, rows, cv), BF16),
            jax.ShapeDtypeStruct((rows, ck), BF16),
            jax.ShapeDtypeStruct((rows, cv), BF16),
            jax.ShapeDtypeStruct((n, rank, rows), BF16),
            jax.ShapeDtypeStruct((1, total), F32),
            jax.ShapeDtypeStruct((n, 1, share), F32),
        ],
        in_specs=[hbm] * 11,
        out_specs=[hbm] * 8,
        scratch_shapes=[
            pltpu.VMEM((rank, rows), BF16), pltpu.VMEM((rank, rows), BF16), pltpu.VMEM((rank, rows), BF16),
            pltpu.VMEM((rank, cq), BF16), pltpu.VMEM((rank, ck), BF16), pltpu.VMEM((rank, cv), BF16),
            pltpu.VMEM((1, share), F32), pltpu.VMEM((1, share), F32),
            pltpu.VMEM((1, total), F32), pltpu.VMEM((n, 1, share), F32), dma((8,)), dma((2,)),
            pltpu.VMEM((rows, cq), BF16), pltpu.VMEM((rows, ck), BF16), pltpu.VMEM((rows, cv), BF16),
            pltpu.VMEM((n, 1, length), F32), pltpu.VMEM((1, length), F32),
            dma((n - 1, count)), dma((n - 1, count)), dma((n - 1, count)), dma((n - 1, count)),
            dma((2, n - 1)), dma((2, n - 1)), dma((2, n - 1)), dma((2, n - 1)),
            dma((3,)), dma((3,)), dma,
        ],
        compiler_params=pltpu.CompilerParams(collective_id=0, has_side_effects=True),
    )(wq, wk, wv, lq.T, lk.T, lv.T, hq, hk, hv, nt.reshape(1, share), ns.reshape(1, share))

    ends = [(1, 0), (n - 2, n - 1)]
    came_k = lax.ppermute(tail_k, "fsdp", ends)
    came_v = lax.ppermute(tail_v, "fsdp", ends)

    glow, norm = pl.pallas_call(
        functools.partial(plane_kernel, m),
        out_shape=[
            jax.ShapeDtypeStruct((3, n, rank, rows), BF16),
            jax.ShapeDtypeStruct((n, m, 1, share), F32),
        ],
        in_specs=[vmem] * 2,
        out_specs=[hbm] * 2,
        scratch_shapes=[dma((3, m - 1)), dma((3,)), dma((m - 1,)), dma((m - 1,)), dma((2,))],
        compiler_params=pltpu.CompilerParams(
            collective_id=1, has_side_effects=True, vmem_limit_bytes=8 * 2**20),
        cost_estimate=pl.CostEstimate(
            flops=2 * n * rows * total * rank, bytes_accessed=n * rows * total, transcendentals=0),
    )(part, normz)

    tile = 128 if rows % 128 == 0 else rows
    halves = 2 if min(cq, ck, cv) % 256 == 0 and ck == cv and cq % ck == 0 else 1
    starts = (0, cq, cq + ck)
    widths = (cq // halves, ck // halves, cv // halves)

    def block(width):
        return pl.BlockSpec((1, rows, width), lambda j, i: (i, 0, j))

    def placed(width):
        return pl.BlockSpec((rows, width), lambda j, i: (i, j))

    def columns(height, width):
        return pl.BlockSpec((height, width), lambda j, i: (0, j))

    def scales(start, width):
        return pl.BlockSpec((1, width), lambda j, i: (0, start // width + j))

    fq, before_k, before_v, col_q, col_k, col_v = pl.pallas_call(
        functools.partial(merge_kernel, tile),
        grid=(halves, n),
        out_shape=[jax.ShapeDtypeStruct((n * rows, c), BF16) for c in (cq, ck, cv)]
        + [jax.ShapeDtypeStruct((1, c), F32) for c in (cq, ck, cv)],
        in_specs=[block(c) for c in widths]
        + [pl.BlockSpec((3, 1, rank, rows), lambda j, i: (0, i, 0, 0))]
        + [columns(rank, c) for c in widths]
        + [scales(start, c) for start, c in zip(starts, widths)],
        out_specs=[placed(c) for c in widths] + [columns(1, c) for c in widths],
        compiler_params=pltpu.CompilerParams(vmem_limit_bytes=60 * 2**20),
        cost_estimate=pl.CostEstimate(
            flops=2 * n * rows * total * rank, bytes_accessed=4 * n * rows * total, transcendentals=0),
    )(gq, gk, gv, glow, hq, hk, hv, col, col, col)

    parts = 7 if rows % (7 * 128) == 0 else 1

    def finish(i, came, tail, high, before):
        width = high.shape[1]
        start = starts[i]
        return pl.pallas_call(
            functools.partial(last_kernel, n, parts),
            grid=(1,),
            out_shape=jax.ShapeDtypeStruct((n * rows, width), BF16),
            in_specs=[vmem, vmem,
                      pl.BlockSpec((1, 1, rank, rows), lambda t: (i, 0, 0, 0)),
                      pl.BlockSpec((1, 1, rank, rows), lambda t: (i, n - 1, 0, 0)),
                      vmem,
                      pl.BlockSpec((1, width), lambda t: (0, start // width)), hbm],
            out_specs=hbm,
            scratch_shapes=[pltpu.VMEM((rows, width), BF16), dma((parts,))],
            input_output_aliases={6: 0},
            compiler_params=pltpu.CompilerParams(vmem_limit_bytes=12 * 2**20),
            cost_estimate=pl.CostEstimate(
                flops=2 * rows * width * rank, bytes_accessed=4 * rows * width, transcendentals=0),
        )(came, tail, glow, glow, high, col, before)

    fk = finish(1, came_k, tail_k, hk, before_k)
    fv = finish(2, came_v, tail_v, hv, before_v)
    return (fq, fk, fv, col_q[0], col_k[0], col_v[0], norm.reshape(-1).astype(BF16))


def solution(mesh):
    placed = (
        P(("trial", "fsdp"), "width"), P(("trial", "fsdp"), None), P("trial", "width"),
        P(("trial", "fsdp"), "width"), P(("trial", "fsdp"), None), P("trial", "width"),
        P(("trial", "fsdp"), "width"), P(("trial", "fsdp"), None), P("trial", "width"),
        P(("trial", "fsdp", "width")), P(("trial", "fsdp", "width")),
    )
    return jax.shard_map(
        functools.partial(local, mesh.shape["fsdp"], mesh.shape["width"]),
        mesh=mesh,
        in_specs=placed,
        out_specs=(
            P("trial", "width"), P("trial", "width"), P("trial", "width"),
            P(("trial", "width")), P(("trial", "width")), P(("trial", "width")),
            P("trial"),
        ),
        check_vma=False,
    )
```

time: 258 us -> 250 us (0.969); the launches traced: 255 us -> 250 us
  Pallas kernels: 249 us -> 234 us
  waiting for transfers between devices: 2.01 us -> 9.62 us
    pallas_call x2 -> x4, Pallas kernels: 230 us -> 215 us  [the longest x1 206 us: local(): pl.pallas_call(functools.partial(line_kernel, n, m), out_shape=[jax.Shape...]
    ppermute x1 -> x2, waiting for transfers between devices: 2.01 us -> 9.62 us  [the longest x1 9.62 us: local(): came_v = lax.ppermute(tail_v, 'fsdp', ends)]
  transfers between devices with their start and end apart: 1 -> 2, of which waited for: 1 -> 1; matrix products, arithmetic and copies ran while one was open for 1% -> 0% of each run, Pallas kernels for 7% -> 11%
where the time goes in v1:
time: 250 us
  Pallas kernels  234 us (94%)
  waiting for transfers between devices  9.62 us (4%)
  local copies, waits for them, and re-layouts  3.01 us (1%)
  starting transfers between devices  2.58 us (1%)
    pallas_call x1, Pallas kernels, local(): pl.pallas_call(functools.partial(line_kernel, n, m), out_shape=[jax.Shape...  206 us
    pallas_call x1, Pallas kernels, local(): pl.pallas_call(functools.partial(merge_kernel, tile), grid=(halves, n), o...  18.5 us
    ppermute x1, waiting for transfers between devices, local(): came_v = lax.ppermute(tail_v, 'fsdp', ends)  9.62 us
    pallas_call x1, Pallas kernels, local(): pl.pallas_call(functools.partial(plane_kernel, m), out_shape=[jax.ShapeDt...  7.19 us
  transfers between devices with their start and end apart: 2, of which 1 were waited for; matrix products, arithmetic and copies ran while one was open for 0% of the time, Pallas kernels for 11%

profile of v1, /device:TPU:4, one launch (start us, length us, event | category | flops | bytes accessed | tf_op | source)
XLA Modules:
  0.0 250.0 jit_solution(17025291962442754812)
XLA Ops:
  0.6 205.8 %shard_map.162 = (bf16[4,896,1024]{2,1,0:T(8,128)(2,1)}, bf16[4,896,512]{2,1,0:T(8,128)(2,1)}, bf16[4,896,512]{2,1,0:T(8,128)(2,1)}, bf16[896,512]{1,0:T(8,128)(...) custom-call(bf16[896,1024]{1,0:T(8,128)(2,1)} %wq.1, ...), custom_call_target="tpu_custom_call" | custom-call | tf_op jit(solution)/shard_map/pallas_call | solution.py:341
  206.5 1.3 collective-permute-start
  207.8 1.3 collective-permute-start.1
  209.1 0.0 copy-start.7
  209.1 0.9 copy-done.7
  210.0 0.0 copy-start.8
  210.0 0.7 copy-done.8
  210.6 7.2 %shard_map.163 = (bf16[3,4,16,896]{3,2,1,0:T(8,128)(2,1)S(1)}, f32[4,4,1,224]{3,2,1,0:T(1,128)S(1)}) custom-call(bf16[4,16,896]{2,1,0:T(8,128)(2,1)S(1)} %copy-done.7, f32[4,1,224]{2,1,0:T(1,128)S(1)} %copy-done.8), custom_call_target="tpu_custom_call" | custom-call | flops 234881024 | bytes 7340032 | tf_op jit(solution)/shard_map/pallas_call | solution.py:373
  217.8 0.0 copy-start
  217.8 0.7 copy-done
  218.6 0.1 convert_reduce_fusion
  218.6 0.7 convert_element_type.7
  219.3 0.0 copy-start.1
  219.3 0.0 copy-start.3
  219.3 0.0 copy-start.4
  219.3 0.0 copy-start.5
  219.3 18.5 %shard_map.164 = (bf16[3584,1024]{1,0:T(8,128)(2,1)}, bf16[3584,512]{1,0:T(8,128)(2,1)}, bf16[3584,512]{1,0:T(8,128)(2,1)}, f32[1,1024]{1,0:T(1,128)}, f32[1,512]{1,0:T(1,128)}, /*index=5*/f32[1,512]{1,0:T(1,128)}) custom-call(bf16[4,896,1024]{2,1,0:T(8,128)(2,1)} %get-tuple-element.23.gq, bf16[4,896,512]{2,1,0:T(8,128)(2,1)} %get-tuple-element.24.gk, ...), custom_call_target="tpu_custom_call" | custom-call | flops 234881024 | bytes 29360128 | tf_op jit(solution)/shard_map/pallas_call | solution.py:405
  237.9 0.0 collective-permute-done.came
  237.9 0.0 copy-done.1
  237.9 0.0 copy-done.3
  237.9 0.0 copy-done.4
  237.9 0.0 copy-done.5
  237.9 0.0 copy-start.2
  237.9 0.0 copy-start.6
  237.9 1.2 shard_map.165
  239.2 9.6 %collective-permute-done.1.came = bf16[896,512]{1,0:T(8,128)(2,1)S(1)} collective-permute-done((bf16[896,512]{1,0:T(8,128)(2,1)}, bf16[896,512]{1,0:T(8,128)(2,1)S(1)}, u32[]{:S(2)}, u32[]{:S(2)}) %collective-permute-start.1) | collective-permute-done | bytes 917536 | tf_op jit(solution)/shard_map/ppermute | solution.py:371
  248.8 0.0 copy-done.2
  248.8 0.0 copy-done.6
  248.8 1.2 shard_map.166
Async XLA Ops:
  206.5 31.4 %collective-permute-start = (bf16[896,512]{1,0:T(8,128)(2,1)}, bf16[896,512]{1,0:T(8,128)(2,1)S(1)}, u32[]{:S(2)}, u32[]{:S(2)}) collective-permute-start(bf16[896,512]{1,0:T(8,128)(2,1)} %get-tuple-element.31.tail), channel_id=1, source_target_pairs={{8,0},{16,24},{9,1},{17,25},{10,2},{18,26},{11,3},{19,27},{12,4},{... | collective-permute-start | bytes 2752520 | tf_op jit(solution)/shard_map/ppermute | solution.py:370
  207.8 41.0 %collective-permute-start.1 = (bf16[896,512]{1,0:T(8,128)(2,1)}, bf16[896,512]{1,0:T(8,128)(2,1)S(1)}, u32[]{:S(2)}, u32[]{:S(2)}) collective-permute-start(bf16[896,512]{1,0:T(8,128)(2,1)} %get-tuple-element.33.tail), channel_id=1, source_target_pairs={{8,0},{16,24},{9,1},{17,25},{10,2},{18,26},{11,3},{19,27},{12,4},{... | collective-permute-start | bytes 2752520 | tf_op jit(solution)/shard_map/ppermute | solution.py:371
  209.1 0.9 copy-start.7
  210.0 0.7 copy-start.8
  217.8 0.7 copy-start
  219.3 18.6 %copy-start.1 = (bf16[3,4,16,896]{3,2,1,0:T(8,128)(2,1)S(1)}, bf16[3,4,16,896]{3,2,1,0:T(8,128)(2,1)}, u32[]{:S(2)}) copy-start(bf16[3,4,16,896]{3,2,1,0:T(8,128)(2,1)} %copy-done) | copy-start | bytes 1032196
  219.3 18.6 %copy-start.3 = (bf16[896,512]{1,0:T(8,128)(2,1)S(1)}, bf16[896,512]{1,0:T(8,128)(2,1)}, u32[]{:S(2)}) copy-start(bf16[896,512]{1,0:T(8,128)(2,1)} %get-tuple-element.31.tail) | copy-start | bytes 2752516
  219.3 18.6 %copy-start.4 = (f32[1,2048]{1,0:T(1,128)S(1)}, f32[1,2048]{1,0:T(1,128)}, u32[]{:S(2)}) copy-start(f32[1,2048]{1,0:T(1,128)} %get-tuple-element.29.col_q.col_k.col_v.col) | copy-start | bytes 24580
  219.3 18.6 %copy-start.5 = (bf16[16,512]{1,0:T(8,128)(2,1)S(1)}, bf16[16,512]{1,0:T(8,128)(2,1)}, u32[]{:S(2)}) copy-start(bf16[16,512]{1,0:T(8,128)(2,1)} %high.2) | copy-start | bytes 49156
  237.9 10.9 %copy-start.2 = (bf16[896,512]{1,0:T(8,128)(2,1)S(1)}, bf16[896,512]{1,0:T(8,128)(2,1)}, u32[]{:S(2)}) copy-start(bf16[896,512]{1,0:T(8,128)(2,1)} %get-tuple-element.33.tail) | copy-start | bytes 2752516
  237.9 10.9 %copy-start.6 = (bf16[16,512]{1,0:T(8,128)(2,1)S(1)}, bf16[16,512]{1,0:T(8,128)(2,1)}, u32[]{:S(2)}) copy-start(bf16[16,512]{1,0:T(8,128)(2,1)} %high.3) | copy-start | bytes 49156

commit v2 on v1

--- a/solution.py
+++ b/solution.py
@@ -35,7 +35,7 @@
                 own_q, own_k, own_v, vec, vec_own,
                 send_up, send_dn, recv_up, recv_dn,
                 low_send, low_recv, vec_send, vec_recv,
-                in_sem, out_sem, low_sem):
+                in_sem, out_sem, low_sem, above):
     z, x = lax.axis_index("fsdp"), lax.axis_index("width")
     weights, gathered, owns = (wq, wk, wv), (gq, gk, gv), (own_q, own_k, own_v)
     asides = {1: tail_k, 2: tail_v}
@@ -52,11 +52,6 @@
     ]
 
     barrier = pltpu.get_barrier_semaphore()
-    ends = (z == 0) | (z == n - 1)
-
-    @pl.when(z > 0)
-    def _():
-        pl.semaphore_signal(barrier, inc=1, device_id_type=MESH, device_id={"fsdp": jnp.maximum(z - 1, 0)})
 
     @pl.when(z < n - 1)
     def _():
@@ -64,14 +59,6 @@
 
     for copy in loads + smalls:
         copy.start()
-
-    @pl.when(ends)
-    def _():
-        pl.semaphore_wait(barrier, 1)
-
-    @pl.when(jnp.logical_not(ends))
-    def _():
-        pl.semaphore_wait(barrier, 2)
 
     def sent_block(hop, up):
         return jnp.clip(z - (hop - 1) if up else z + (hop - 1), 0, n - 1)
@@ -138,9 +125,20 @@
     def carried(i):
         return x == carrier(i, m)
 
+    @pl.when(z > 0)
+    def _():
+        pl.semaphore_wait(barrier, 1)
+        pl.semaphore_signal(above, inc=1, device_id_type=MESH, device_id={"fsdp": jnp.maximum(z - 1, 0)})
+
     for c in range(count):
-        for up in WAYS:
-            start_piece(1, c, up)
+        start_piece(1, c, False)
+
+    @pl.when(z < n - 1)
+    def _():
+        pl.semaphore_wait(above, 1)
+
+    for c in range(count):
+        start_piece(1, c, True)
     for i in range(3):
         for up in WAYS:
             @pl.when(carried(i) & sends(1, up))
@@ -361,7 +359,7 @@
             pltpu.VMEM((n, 1, length), F32), pltpu.VMEM((1, length), F32),
             dma((n - 1, count)), dma((n - 1, count)), dma((n - 1, count)), dma((n - 1, count)),
             dma((2, n - 1)), dma((2, n - 1)), dma((2, n - 1)), dma((2, n - 1)),
-            dma((3,)), dma((3,)), dma,
+            dma((3,)), dma((3,)), dma, pltpu.SemaphoreType.REGULAR,
         ],
         compiler_params=pltpu.CompilerParams(collective_id=0, has_side_effects=True),
     )(wq, wk, wv, lq.T, lk.T, lv.T, hq, hk, hv, nt.reshape(1, share), ns.reshape(1, share))

time: 250 us -> 249 us (level)
  no operation moved by 1% of the time
where the time goes in v2:
time: 249 us
  Pallas kernels  233 us (94%)
  waiting for transfers between devices  9.45 us (4%)
  local copies, waits for them, and re-layouts  3.01 us (1%)
  starting transfers between devices  2.58 us (1%)
    pallas_call x1, Pallas kernels, local(): pl.pallas_call(functools.partial(line_kernel, n, m), out_shape=[jax.Shape...  205 us
    pallas_call x1, Pallas kernels, local(): pl.pallas_call(functools.partial(merge_kernel, tile), grid=(halves, n), o...  18.5 us
    ppermute x1, waiting for transfers between devices, local(): came_v = lax.ppermute(tail_v, 'fsdp', ends)  9.45 us
    pallas_call x1, Pallas kernels, local(): pl.pallas_call(functools.partial(plane_kernel, m), out_shape=[jax.ShapeDt...  7.19 us
  transfers between devices with their start and end apart: 2, of which 1 were waited for; matrix products, arithmetic and copies ran while one was open for 0% of the time, Pallas kernels for 11%

profile of v2, /device:TPU:4, one launch (start us, length us, event | category | flops | bytes accessed | tf_op | source)
XLA Modules:
  0.0 248.7 jit_solution(3252584601203484415)
XLA Ops:
  0.6 204.7 %shard_map.162 = (bf16[4,896,1024]{2,1,0:T(8,128)(2,1)}, bf16[4,896,512]{2,1,0:T(8,128)(2,1)}, bf16[4,896,512]{2,1,0:T(8,128)(2,1)}, bf16[896,512]{1,0:T(8,128)(...) custom-call(bf16[896,1024]{1,0:T(8,128)(2,1)} %wq.1, ...), custom_call_target="tpu_custom_call" | custom-call | tf_op jit(solution)/shard_map/pallas_call | solution.py:339
  205.3 1.3 collective-permute-start
  206.6 1.3 collective-permute-start.1
  207.9 0.0 copy-start.7
  207.9 0.9 copy-done.7
  208.8 0.0 copy-start.8
  208.8 0.7 copy-done.8
  209.5 7.2 %shard_map.163 = (bf16[3,4,16,896]{3,2,1,0:T(8,128)(2,1)S(1)}, f32[4,4,1,224]{3,2,1,0:T(1,128)S(1)}) custom-call(bf16[4,16,896]{2,1,0:T(8,128)(2,1)S(1)} %copy-done.7, f32[4,1,224]{2,1,0:T(1,128)S(1)} %copy-done.8), custom_call_target="tpu_custom_call" | custom-call | flops 234881024 | bytes 7340032 | tf_op jit(solution)/shard_map/pallas_call | solution.py:371
  216.7 0.0 copy-start
  216.7 0.7 copy-done
  217.4 0.1 convert_reduce_fusion
  217.5 0.7 convert_element_type.7
  218.2 0.0 copy-start.1
  218.2 0.0 copy-start.3
  218.2 0.0 copy-start.4
  218.2 0.0 copy-start.5
  218.2 18.5 %shard_map.164 = (bf16[3584,1024]{1,0:T(8,128)(2,1)}, bf16[3584,512]{1,0:T(8,128)(2,1)}, bf16[3584,512]{1,0:T(8,128)(2,1)}, f32[1,1024]{1,0:T(1,128)}, f32[1,512]{1,0:T(1,128)}, /*index=5*/f32[1,512]{1,0:T(1,128)}) custom-call(bf16[4,896,1024]{2,1,0:T(8,128)(2,1)} %get-tuple-element.23.gq, bf16[4,896,512]{2,1,0:T(8,128)(2,1)} %get-tuple-element.24.gk, ...), custom_call_target="tpu_custom_call" | custom-call | flops 234881024 | bytes 29360128 | tf_op jit(solution)/shard_map/pallas_call | solution.py:403
  236.7 0.0 collective-permute-done.came
  236.7 0.0 copy-done.1
  236.7 0.0 copy-done.3
  236.8 0.0 copy-done.4
  236.8 0.0 copy-done.5
  236.8 0.0 copy-start.2
  236.8 0.0 copy-start.6
  236.8 1.2 shard_map.165
  238.0 9.5 %collective-permute-done.1.came = bf16[896,512]{1,0:T(8,128)(2,1)S(1)} collective-permute-done((bf16[896,512]{1,0:T(8,128)(2,1)}, bf16[896,512]{1,0:T(8,128)(2,1)S(1)}, u32[]{:S(2)}, u32[]{:S(2)}) %collective-permute-start.1) | collective-permute-done | bytes 917536 | tf_op jit(solution)/shard_map/ppermute | solution.py:369
  247.5 0.0 copy-done.2
  247.5 0.0 copy-done.6
  247.5 1.2 shard_map.166
Async XLA Ops:
  205.3 31.4 %collective-permute-start = (bf16[896,512]{1,0:T(8,128)(2,1)}, bf16[896,512]{1,0:T(8,128)(2,1)S(1)}, u32[]{:S(2)}, u32[]{:S(2)}) collective-permute-start(bf16[896,512]{1,0:T(8,128)(2,1)} %get-tuple-element.31.tail), channel_id=1, source_target_pairs={{8,0},{16,24},{9,1},{17,25},{10,2},{18,26},{11,3},{19,27},{12,4},{... | collective-permute-start | bytes 2752520 | tf_op jit(solution)/shard_map/ppermute | solution.py:368
  206.6 40.9 %collective-permute-start.1 = (bf16[896,512]{1,0:T(8,128)(2,1)}, bf16[896,512]{1,0:T(8,128)(2,1)S(1)}, u32[]{:S(2)}, u32[]{:S(2)}) collective-permute-start(bf16[896,512]{1,0:T(8,128)(2,1)} %get-tuple-element.33.tail), channel_id=1, source_target_pairs={{8,0},{16,24},{9,1},{17,25},{10,2},{18,26},{11,3},{19,27},{12,4},{... | collective-permute-start | bytes 2752520 | tf_op jit(solution)/shard_map/ppermute | solution.py:369
  207.9 0.9 copy-start.7
  208.8 0.7 copy-start.8
  216.7 0.7 copy-start
  218.2 18.6 %copy-start.1 = (bf16[3,4,16,896]{3,2,1,0:T(8,128)(2,1)S(1)}, bf16[3,4,16,896]{3,2,1,0:T(8,128)(2,1)}, u32[]{:S(2)}) copy-start(bf16[3,4,16,896]{3,2,1,0:T(8,128)(2,1)} %copy-done) | copy-start | bytes 1032196
  218.2 18.6 %copy-start.3 = (bf16[896,512]{1,0:T(8,128)(2,1)S(1)}, bf16[896,512]{1,0:T(8,128)(2,1)}, u32[]{:S(2)}) copy-start(bf16[896,512]{1,0:T(8,128)(2,1)} %get-tuple-element.31.tail) | copy-start | bytes 2752516
  218.2 18.6 %copy-start.4 = (f32[1,2048]{1,0:T(1,128)S(1)}, f32[1,2048]{1,0:T(1,128)}, u32[]{:S(2)}) copy-start(f32[1,2048]{1,0:T(1,128)} %get-tuple-element.29.col_q.col_k.col_v.col) | copy-start | bytes 24580
  218.2 18.6 %copy-start.5 = (bf16[16,512]{1,0:T(8,128)(2,1)S(1)}, bf16[16,512]{1,0:T(8,128)(2,1)}, u32[]{:S(2)}) copy-start(bf16[16,512]{1,0:T(8,128)(2,1)} %high.2) | copy-start | bytes 49156
  236.8 10.7 %copy-start.2 = (bf16[896,512]{1,0:T(8,128)(2,1)S(1)}, bf16[896,512]{1,0:T(8,128)(2,1)}, u32[]{:S(2)}) copy-start(bf16[896,512]{1,0:T(8,128)(2,1)} %get-tuple-element.33.tail) | copy-start | bytes 2752516
  236.8 10.7 %copy-start.6 = (bf16[16,512]{1,0:T(8,128)(2,1)S(1)}, bf16[16,512]{1,0:T(8,128)(2,1)}, u32[]{:S(2)}) copy-start(bf16[16,512]{1,0:T(8,128)(2,1)} %high.3) | copy-start | bytes 49156

commit v3 on v2

--- a/solution.py
+++ b/solution.py
@@ -7,6 +7,7 @@
 from jax.experimental.pallas import tpu as pltpu
 from jax.sharding import PartitionSpec as P
 
+
 mix_rate = 2.0
 MESH = pl.DeviceIdType.MESH
 F32, BF16 = jnp.float32, jnp.bfloat16
@@ -15,21 +16,26 @@
 
 def pieces_of(rows, widths):
     smallest = min(widths)
+    unit = 128 if rows % 128 == 0 else 8
+    units = rows // unit
     pieces = []
     for a, width in enumerate(widths):
-        count = 2 * (width // smallest)
-        while rows % (count * 8):
-            count //= 2
-        pieces += [(a, i * (rows // count), rows // count) for i in range(count)]
+        count = min(2 * (width // smallest), units)
+        cuts = [unit * (i * units // count) for i in range(count + 1)]
+        pieces += [(a, first, last - first) for first, last in zip(cuts, cuts[1:])]
     return pieces
+
+
+def held_of(pieces):
+    return max(c for c, (a, _, _) in enumerate(pieces) if a == 0)
 
 
 def carrier(i, m):
     return (m - 1 - i) % m
 
 
-def line_kernel(n, m, wq, wk, wv, lq, lk, lv, hq, hk, hv, nt, ns,
-                gq, gk, gv, tail_k, tail_v, glow, col_out, norm_out,
+def line_kernel(n, m, trials, wq, wk, wv, lq, lk, lv, hq, hk, hv, nt, ns,
+                gq, gk, gv, tail_q, tail_k, tail_v, glow, col_out, norm_out,
                 low_q, low_k, low_v, high_q, high_k, high_v, train, step_v, col_ref, norm_ref,
                 small_sem, result_sem,
                 own_q, own_k, own_v, vec, vec_own,
@@ -38,12 +44,14 @@
                 in_sem, out_sem, low_sem, above):
     z, x = lax.axis_index("fsdp"), lax.axis_index("width")
     weights, gathered, owns = (wq, wk, wv), (gq, gk, gv), (own_q, own_k, own_v)
-    asides = {1: tail_k, 2: tail_v}
+    asides = (tail_q, tail_k, tail_v)
+    late = lax.axis_index("trial") == trials - 1
     lows, near_lows, near_highs = (lq, lk, lv), (low_q, low_k, low_v), (high_q, high_k, high_v)
     rows = wq.shape[0]
     share = train.shape[1]
     pieces = pieces_of(rows, [w.shape[1] for w in weights])
     count = len(pieces)
+    spare = held_of(pieces)
 
     loads = [pltpu.make_async_copy(w, o, in_sem.at[i]) for i, (w, o) in enumerate(zip(weights, owns))]
     smalls = [
@@ -75,8 +83,13 @@
     def receives(hop, up):
         return z >= hop if up else z + hop <= n - 1
 
-    def travels(hop, c):
-        return not (hop == n - 1 and pieces[c][0] in asides)
+    def held(c):
+        return late if c == spare else pieces[c][0] > 0
+
+    def travels(hop, c, when):
+        if hop < n - 1 or held(c) is False:
+            return when
+        return False if held(c) is True else when & jnp.logical_not(held(c))
 
     def piece(hop, c, up, aside=False):
         a, first, size = pieces[c]
@@ -84,7 +97,7 @@
         landing = gathered[a].at[block, pl.ds(first, size)]
         source = weights[a].at[pl.ds(first, size)] if hop == 1 else landing
         if aside:
-            landing = asides[a].at[pl.ds(first, size)]
+            landing = asides[a].at[pl.ds(0 if c == spare else first, size)]
         out, back = (send_up, recv_up) if up else (send_dn, recv_dn)
         return pltpu.make_async_remote_copy(
             src_ref=source, dst_ref=landing,
@@ -93,18 +106,23 @@
         )
 
     def start_piece(hop, c, up):
-        if hop == n - 2 and pieces[c][0] in asides:
+        when = travels(hop, c, sends(hop, up))
+        if when is False:
+            return
+        if hop == n - 2 and held(c) is not False:
             aside = (z == n - 3) if up else (z == 2)
-
-            @pl.when(sends(hop, up) & aside)
+            if held(c) is not True:
+                aside = aside & held(c)
+
+            @pl.when(when & aside)
             def _():
                 piece(hop, c, up, True).start()
 
-            @pl.when(sends(hop, up) & jnp.logical_not(aside))
+            @pl.when(when & jnp.logical_not(aside))
             def _():
                 piece(hop, c, up).start()
         else:
-            @pl.when(sends(hop, up))
+            @pl.when(when)
             def _():
                 piece(hop, c, up).start()
 
@@ -196,13 +214,14 @@
                             def _():
                                 low_piece(hop + 1, i, up).start()
         for c in range(count):
-            if not travels(hop, c):
+            if held(c) is True and hop == n - 1:
                 continue
             for up in WAYS:
-                @pl.when(receives(hop, up))
+                @pl.when(travels(hop, c, receives(hop, up)))
                 def _(hop=hop, c=c, up=up):
                     piece(hop, c, up).wait_recv()
-                if hop < n - 1 and travels(hop + 1, c):
+
+                if hop < n - 1:
                     start_piece(hop + 1, c, up)
             if c == 1:
                 for up in WAYS:
@@ -235,9 +254,14 @@
                     @pl.when(carried(i))
                     def _(i=i):
                         low_piece(hop, i, up).wait_send()
-                for c in range(count):
-                    if travels(hop, c):
-                        piece(hop, c, up).wait_send()
+
+            for c in range(count):
+                if held(c) is True and hop == n - 1:
+                    continue
+
+                @pl.when(travels(hop, c, sends(hop, up)))
+                def _(hop=hop, c=c, up=up):
+                    piece(hop, c, up).wait_send()
 
 
 def plane_kernel(m, low_ref, norm_ref, glow, norm, low_send, low_recv, norm_send, norm_recv, own_sem):
@@ -301,47 +325,53 @@
     lax.fori_loop(0, gq.shape[1] // tile, step, 0)
 
 
-def last_kernel(n, parts, came, tail, low_first, low_last, high, col, before, final, out_ref, out_sem):
+def last_kernel(n, first, tile, wanted, came, tail, low_first, low_last, high, col, before, final, out_ref, out_sem):
     z = lax.axis_index("fsdp")
-    rows = came.shape[0]
-    size = rows // parts
+    size = came.shape[0]
+    rows = low_first.shape[3]
 
     def store(p, block):
         return pltpu.make_async_copy(
-            out_ref.at[pl.ds(p * size, size)],
-            final.at[pl.ds(block * rows + p * size, size)], out_sem.at[p])
+            out_ref.at[pl.ds(p * tile, tile)],
+            final.at[pl.ds(block * rows + first + p * tile, tile)], out_sem.at[p])
 
     def write(source, low, block):
         scale = 1.0 / col[...]
-        for p in range(parts):
-            span = pl.ds(p * size, size)
-            out_ref[span, :] = merged(source[span, :], low[0, 0, :, span], high[...], scale)
+        for p in range(size // tile):
+            span = pl.ds(p * tile, tile)
+            out_ref[span, :] = merged(source[span, :], low[0, 0, :, pl.ds(first + p * tile, tile)], high[...], scale)
             store(p, block).start()
-        for p in range(parts):
+        for p in range(size // tile):
             store(p, block).wait()
 
     for at, source, low, block in ((0, came, low_last, n - 1), (1, tail, low_last, n - 1),
                                    (n - 2, tail, low_first, 0), (n - 1, came, low_first, 0)):
-        @pl.when(z == at)
+        here = z == at
+        if wanted is not None:
+            here = here & (lax.axis_index("trial") == wanted)
+
+        @pl.when(here)
         def _(source=source, low=low, block=block):
             write(source, low, block)
 
 
-def local(n, m, wq, lq, hq, wk, lk, hk, wv, lv, hv, nt, ns):
+def local(n, m, trials, wq, lq, hq, wk, lk, hk, wv, lv, hv, nt, ns):
     rows, cq = wq.shape
     ck, cv = wk.shape[1], wv.shape[1]
     rank, share = hq.shape[0], nt.shape[0]
     total = cq + ck + cv
     length = total + -(-share // 128) * 128
-    count = len(pieces_of(rows, [cq, ck, cv]))
+    pieces = pieces_of(rows, [cq, ck, cv])
+    count, spare = len(pieces), held_of(pieces)
     hbm, vmem = pl.BlockSpec(memory_space=pl.ANY), pl.BlockSpec(memory_space=pltpu.VMEM)
     dma = pltpu.SemaphoreType.DMA
-    gq, gk, gv, tail_k, tail_v, part, col, normz = pl.pallas_call(
-        functools.partial(line_kernel, n, m),
+    gq, gk, gv, tail_q, tail_k, tail_v, part, col, normz = pl.pallas_call(
+        functools.partial(line_kernel, n, m, trials),
         out_shape=[
             jax.ShapeDtypeStruct((n, rows, cq), BF16),
             jax.ShapeDtypeStruct((n, rows, ck), BF16),
             jax.ShapeDtypeStruct((n, rows, cv), BF16),
+            jax.ShapeDtypeStruct((pieces[spare][2], cq), BF16),
             jax.ShapeDtypeStruct((rows, ck), BF16),
             jax.ShapeDtypeStruct((rows, cv), BF16),
             jax.ShapeDtypeStruct((n, rank, rows), BF16),
@@ -349,7 +379,7 @@
             jax.ShapeDtypeStruct((n, 1, share), F32),
         ],
         in_specs=[hbm] * 11,
-        out_specs=[hbm] * 8,
+        out_specs=[hbm] * 9,
         scratch_shapes=[
             pltpu.VMEM((rank, rows), BF16), pltpu.VMEM((rank, rows), BF16), pltpu.VMEM((rank, rows), BF16),
             pltpu.VMEM((rank, cq), BF16), pltpu.VMEM((rank, ck), BF16), pltpu.VMEM((rank, cv), BF16),
@@ -365,6 +395,8 @@
     )(wq, wk, wv, lq.T, lk.T, lv.T, hq, hk, hv, nt.reshape(1, share), ns.reshape(1, share))
 
     ends = [(1, 0), (n - 2, n - 1)]
+    lone = [(a * trials + trials - 1, b * trials + trials - 1) for a, b in ends]
+    came_q = lax.ppermute(tail_q, ("fsdp", "trial"), lone)
     came_k = lax.ppermute(tail_k, "fsdp", ends)
     came_v = lax.ppermute(tail_v, "fsdp", ends)
 
@@ -400,7 +432,7 @@
     def scales(start, width):
         return pl.BlockSpec((1, width), lambda j, i: (0, start // width + j))
 
-    fq, before_k, before_v, col_q, col_k, col_v = pl.pallas_call(
+    before_q, before_k, before_v, col_q, col_k, col_v = pl.pallas_call(
         functools.partial(merge_kernel, tile),
         grid=(halves, n),
         out_shape=[jax.ShapeDtypeStruct((n * rows, c), BF16) for c in (cq, ck, cv)]
@@ -415,13 +447,12 @@
             flops=2 * n * rows * total * rank, bytes_accessed=4 * n * rows * total, transcendentals=0),
     )(gq, gk, gv, glow, hq, hk, hv, col, col, col)
 
-    parts = 7 if rows % (7 * 128) == 0 else 1
-
-    def finish(i, came, tail, high, before):
-        width = high.shape[1]
+    def finish(i, came, tail, high, before, first, wanted):
+        size, width = came.shape
+        step = 128 if rows % 128 == 0 else size
         start = starts[i]
         return pl.pallas_call(
-            functools.partial(last_kernel, n, parts),
+            functools.partial(last_kernel, n, first, step, wanted),
             grid=(1,),
             out_shape=jax.ShapeDtypeStruct((n * rows, width), BF16),
             in_specs=[vmem, vmem,
@@ -430,15 +461,16 @@
                       vmem,
                       pl.BlockSpec((1, width), lambda t: (0, start // width)), hbm],
             out_specs=hbm,
-            scratch_shapes=[pltpu.VMEM((rows, width), BF16), dma((parts,))],
+            scratch_shapes=[pltpu.VMEM((size, width), BF16), dma((size // step,))],
             input_output_aliases={6: 0},
             compiler_params=pltpu.CompilerParams(vmem_limit_bytes=12 * 2**20),
             cost_estimate=pl.CostEstimate(
-                flops=2 * rows * width * rank, bytes_accessed=4 * rows * width, transcendentals=0),
+                flops=2 * size * width * rank, bytes_accessed=4 * size * width, transcendentals=0),
         )(came, tail, glow, glow, high, col, before)
 
-    fk = finish(1, came_k, tail_k, hk, before_k)
-    fv = finish(2, came_v, tail_v, hv, before_v)
+    fq = finish(0, came_q, tail_q, hq, before_q, pieces[spare][1], trials - 1)
+    fk = finish(1, came_k, tail_k, hk, before_k, 0, None)
+    fv = finish(2, came_v, tail_v, hv, before_v, 0, None)
     return (fq, fk, fv, col_q[0], col_k[0], col_v[0], norm.reshape(-1).astype(BF16))
 
 
@@ -450,7 +482,7 @@
         P(("trial", "fsdp", "width")), P(("trial", "fsdp", "width")),
     )
     return jax.shard_map(
-        functools.partial(local, mesh.shape["fsdp"], mesh.shape["width"]),
+        functools.partial(local, mesh.shape["fsdp"], mesh.shape["width"], mesh.shape["trial"]),
         mesh=mesh,
         in_specs=placed,
         out_specs=(

time: 249 us -> 245 us (0.984)
  Pallas kernels: 233 us -> 229 us
    pallas_call x3 -> x4, Pallas kernels: 207 us -> 203 us  [the longest x1 200 us: local(): pl.pallas_call(functools.partial(line_kernel, n, m, trials), out_shape=[j...]
  transfers between devices with their start and end apart: 2 -> 3, of which waited for: 1 -> 1; matrix products, arithmetic and copies ran while one was open for 0% -> 0% of each run, Pallas kernels for 11% -> 11%
where the time goes in v3:
time: 245 us; the launch traced here: 244 us
  Pallas kernels  229 us (93%)
  waiting for transfers between devices  7.63 us (3%)
  local copies, waits for them, and re-layouts  4.1 us (2%)
  starting transfers between devices  3.28 us (1%)
    pallas_call x1, Pallas kernels, local(): pl.pallas_call(functools.partial(line_kernel, n, m, trials), out_shape=[j...  200 us
    pallas_call x1, Pallas kernels, local(): pl.pallas_call(functools.partial(merge_kernel, tile), grid=(halves, n), o...  18.5 us
    ppermute x1, waiting for transfers between devices, local(): came_v = lax.ppermute(tail_v, 'fsdp', ends)  7.63 us
    pallas_call x1, Pallas kernels, local(): pl.pallas_call(functools.partial(plane_kernel, m), out_shape=[jax.ShapeDt...  7.19 us
  transfers between devices with their start and end apart: 3, of which 1 were waited for; matrix products, arithmetic and copies ran while one was open for 0% of the time, Pallas kernels for 11%

profile of v3, /device:TPU:4, one launch (start us, length us, event | category | flops | bytes accessed | tf_op | source)
XLA Modules:
  0.0 244.4 jit_solution(15949685397594648355)
XLA Ops:
  0.6 200.4 %shard_map.162 = (bf16[4,896,1024]{2,1,0:T(8,128)(2,1)}, bf16[4,896,512]{2,1,0:T(8,128)(2,1)}, bf16[4,896,512]{2,1,0:T(8,128)(2,1)}, bf16[256,1024]{1,0:T(8,128)...) custom-call(bf16[896,1024]{1,0:T(8,128)(2,1)} %wq.1, ...), custom_call_target="tpu_custom_call" | custom-call | tf_op jit(solution)/shard_map/pallas_call | solution.py:368
  201.0 1.3 collective-permute-start.1
  202.3 1.3 collective-permute-start.2
  203.6 0.7 collective-permute-start
  204.3 0.0 copy-start.9
  204.3 0.9 copy-done.9
  205.2 0.0 copy-start.10
  205.2 0.7 copy-done.10
  205.9 7.2 %shard_map.163 = (bf16[3,4,16,896]{3,2,1,0:T(8,128)(2,1)S(1)}, f32[4,4,1,224]{3,2,1,0:T(1,128)S(1)}) custom-call(bf16[4,16,896]{2,1,0:T(8,128)(2,1)S(1)} %copy-done.9, f32[4,1,224]{2,1,0:T(1,128)S(1)} %copy-done.10), custom_call_target="tpu_custom_call" | custom-call | flops 234881024 | bytes 7340032 | tf_op jit(solution)/shard_map/pallas_call | solution.py:403
  213.1 0.0 copy-start
  213.1 0.7 copy-done
  213.8 0.1 convert_reduce_fusion
  213.9 0.7 convert_element_type.7
  214.6 0.0 copy-start.1
  214.6 0.0 copy-start.4
  214.6 18.5 %shard_map.164 = (bf16[3584,1024]{1,0:T(8,128)(2,1)}, bf16[3584,512]{1,0:T(8,128)(2,1)}, bf16[3584,512]{1,0:T(8,128)(2,1)}, f32[1,1024]{1,0:T(1,128)}, f32[1,512]{1,0:T(1,128)}, /*index=5*/f32[1,512]{1,0:T(1,128)}) custom-call(bf16[4,896,1024]{2,1,0:T(8,128)(2,1)} %get-tuple-element.29.gq, bf16[4,896,512]{2,1,0:T(8,128)(2,1)} %get-tuple-element.30.gk, ...), custom_call_target="tpu_custom_call" | custom-call | flops 234881024 | bytes 29360128 | tf_op jit(solution)/shard_map/pallas_call | solution.py:435
  233.1 0.0 collective-permute-done.came
  233.1 0.0 copy-done.1
  233.1 0.0 copy-done.4
  233.2 0.0 copy-done.5
  233.2 0.0 copy-done.6
  233.2 0.0 copy-start.3
  233.2 0.0 copy-start.7
  233.2 0.1 shard_map.165
  233.3 0.0 collective-permute-done.1.came
  233.3 1.1 copy-done.3
  234.4 0.0 copy-done.7
  234.4 1.2 shard_map.166
  235.6 7.6 %collective-permute-done.2.came = bf16[896,512]{1,0:T(8,128)(2,1)S(1)} collective-permute-done((bf16[896,512]{1,0:T(8,128)(2,1)}, bf16[896,512]{1,0:T(8,128)(2,1)S(1)}, u32[]{:S(2)}, u32[]{:S(2)}) %collective-permute-start.2) | collective-permute-done | bytes 917536 | tf_op jit(solution)/shard_map/ppermute | solution.py:401
  243.2 0.0 copy-done.2
  243.2 0.0 copy-done.8
  243.2 1.2 shard_map.167
  (4 shorter events, 0.0 us)
Async XLA Ops:
  201.0 32.2 %collective-permute-start.1 = (bf16[896,512]{1,0:T(8,128)(2,1)}, bf16[896,512]{1,0:T(8,128)(2,1)S(1)}, u32[]{:S(2)}, u32[]{:S(2)}) collective-permute-start(bf16[896,512]{1,0:T(8,128)(2,1)} %get-tuple-element.33.tail), channel_id=1, source_target_pairs={{8,0},{16,24},{9,1},{17,25},{10,2},{18,26},{11,3},{19,27},{12,4},{... | collective-permute-start | bytes 2752520 | tf_op jit(solution)/shard_map/ppermute | solution.py:400
  202.3 40.9 %collective-permute-start.2 = (bf16[896,512]{1,0:T(8,128)(2,1)}, bf16[896,512]{1,0:T(8,128)(2,1)S(1)}, u32[]{:S(2)}, u32[]{:S(2)}) collective-permute-start(bf16[896,512]{1,0:T(8,128)(2,1)} %get-tuple-element.35.tail), channel_id=1, source_target_pairs={{8,0},{16,24},{9,1},{17,25},{10,2},{18,26},{11,3},{19,27},{12,4},{... | collective-permute-start | bytes 2752520 | tf_op jit(solution)/shard_map/ppermute | solution.py:401
  203.6 29.5 %collective-permute-start = (bf16[256,1024]{1,0:T(8,128)(2,1)}, bf16[256,1024]{1,0:T(8,128)(2,1)S(1)}, u32[]{:S(2)}, u32[]{:S(2)}) collective-permute-start(bf16[256,1024]{1,0:T(8,128)(2,1)} %get-tuple-element.24.tail), channel_id=1, source_target_pairs={{9,1},{17,25},{11,3},{19,27},{13,5},{21,29},{15,7},{23,31}} | collective-permute-start | bytes 1572872 | tf_op jit(solution)/shard_map/ppermute | solution.py:399
  204.3 0.9 copy-start.9
  205.2 0.7 copy-start.10
  213.1 0.7 copy-start
  214.6 18.6 %copy-start.1 = (bf16[3,4,16,896]{3,2,1,0:T(8,128)(2,1)S(1)}, bf16[3,4,16,896]{3,2,1,0:T(8,128)(2,1)}, u32[]{:S(2)}) copy-start(bf16[3,4,16,896]{3,2,1,0:T(8,128)(2,1)} %copy-done) | copy-start | bytes 1032196
  214.6 18.6 %copy-start.4 = (bf16[256,1024]{1,0:T(8,128)(2,1)S(1)}, bf16[256,1024]{1,0:T(8,128)(2,1)}, u32[]{:S(2)}) copy-start(bf16[256,1024]{1,0:T(8,128)(2,1)} %get-tuple-element.24.tail) | copy-start | bytes 1572868
  214.6 18.6 %copy-start.5 = (bf16[16,1024]{1,0:T(8,128)(2,1)S(1)}, bf16[16,1024]{1,0:T(8,128)(2,1)}, u32[]{:S(2)}) copy-start(bf16[16,1024]{1,0:T(8,128)(2,1)} %high.3) | copy-start | bytes 98308
  214.6 18.6 %copy-start.6 = (f32[1,2048]{1,0:T(1,128)S(1)}, f32[1,2048]{1,0:T(1,128)}, u32[]{:S(2)}) copy-start(f32[1,2048]{1,0:T(1,128)} %get-tuple-element.28.col_q.col_k.col_v.col) | copy-start | bytes 24580
  233.2 1.2 copy-start.3
  233.2 1.2 copy-start.7
  234.4 8.8 %copy-start.2 = (bf16[896,512]{1,0:T(8,128)(2,1)S(1)}, bf16[896,512]{1,0:T(8,128)(2,1)}, u32[]{:S(2)}) copy-start(bf16[896,512]{1,0:T(8,128)(2,1)} %get-tuple-element.35.tail) | copy-start | bytes 2752516
  234.4 8.8 %copy-start.8 = (bf16[16,512]{1,0:T(8,128)(2,1)S(1)}, bf16[16,512]{1,0:T(8,128)(2,1)}, u32[]{:S(2)}) copy-start(bf16[16,512]{1,0:T(8,128)(2,1)} %high.5) | copy-start | bytes 49156

commit v4 on v3

--- a/solution.py
+++ b/solution.py
@@ -148,20 +148,24 @@
         pl.semaphore_wait(barrier, 1)
         pl.semaphore_signal(above, inc=1, device_id_type=MESH, device_id={"fsdp": jnp.maximum(z - 1, 0)})
 
-    for c in range(count):
+    def start_low(up):
+        for i in range(3):
+            @pl.when(carried(i) & sends(1, up))
+            def _(i=i):
+                low_piece(1, i, up).start()
+
+    lead = min(3, count)
+    for c in range(lead):
         start_piece(1, c, False)
+    start_low(False)
 
     @pl.when(z < n - 1)
     def _():
         pl.semaphore_wait(above, 1)
 
-    for c in range(count):
+    for c in range(lead):
         start_piece(1, c, True)
-    for i in range(3):
-        for up in WAYS:
-            @pl.when(carried(i) & sends(1, up))
-            def _(i=i, up=up):
-                low_piece(1, i, up).start()
+    start_low(True)
 
     for small in smalls:
         small.wait()
@@ -199,12 +203,22 @@
         def _(up=up):
             vec_piece(1, up).start()
 
+    for c in range(lead, count):
+        for up in (False, True):
+            start_piece(1, c, up)
+
     results = [pltpu.make_async_copy(col_ref, col_out, result_sem.at[0]),
                pltpu.make_async_copy(norm_ref, norm_out, result_sem.at[1])]
-    for hop in range(1, n):
+
+    def small_turn(hop):
         for up in WAYS:
             @pl.when(receives(hop, up))
-            def _(hop=hop, up=up):
+            def _(up=up):
+                vec_piece(hop, up).wait_recv()
+                if hop < n - 1:
+                    @pl.when(sends(hop + 1, up))
+                    def _():
+                        vec_piece(hop + 1, up).start()
                 for i in range(3):
                     @pl.when(carried(i))
                     def _(i=i):
@@ -213,6 +227,16 @@
                             @pl.when(sends(hop + 1, up))
                             def _():
                                 low_piece(hop + 1, i, up).start()
+                block = came_block(hop, up)
+                came = vec[block]
+                col_ref[...] = jnp.maximum(col_ref[...], came[:, :total])
+                norm_ref[block] = came[:, total:total + share]
+        if hop == n - 1:
+            for result in results:
+                result.start()
+
+    turn = min(3, spare)
+    for hop in range(1, n):
         for c in range(count):
             if held(c) is True and hop == n - 1:
                 continue
@@ -223,22 +247,8 @@
 
                 if hop < n - 1:
                     start_piece(hop + 1, c, up)
-            if c == 1:
-                for up in WAYS:
-                    @pl.when(receives(hop, up))
-                    def _(hop=hop, up=up):
-                        vec_piece(hop, up).wait_recv()
-                        if hop < n - 1:
-                            @pl.when(sends(hop + 1, up))
-                            def _():
-                                vec_piece(hop + 1, up).start()
-                        block = came_block(hop, up)
-                        came = vec[block]
-                        col_ref[...] = jnp.maximum(col_ref[...], came[:, :total])
-                        norm_ref[block] = came[:, total:total + share]
-                if hop == n - 1:
-                    for result in results:
-                        result.start()
+            if c == turn:
+                small_turn(hop)
     for copy in stores + results:
         copy.wait()
     for i in range(3):

time: 245 us -> 244 us (level)
  Pallas kernels: 229 us -> 226 us
where the time goes in v4:
time: 244 us; the launch traced here: 243 us
  Pallas kernels  226 us (93%)
  waiting for transfers between devices  8.47 us (3%)
  local copies, waits for them, and re-layouts  4.1 us (2%)
  starting transfers between devices  3.28 us (1%)
    pallas_call x1, Pallas kernels, local(): pl.pallas_call(functools.partial(line_kernel, n, m, trials), out_shape=[j...  198 us
    pallas_call x1, Pallas kernels, local(): pl.pallas_call(functools.partial(merge_kernel, tile), grid=(halves, n), o...  18.5 us
    ppermute x1, waiting for transfers between devices, local(): came_v = lax.ppermute(tail_v, 'fsdp', ends)  8.47 us
    pallas_call x1, Pallas kernels, local(): pl.pallas_call(functools.partial(plane_kernel, m), out_shape=[jax.ShapeDt...  7.19 us
  transfers between devices with their start and end apart: 3, of which 1 were waited for; matrix products, arithmetic and copies ran while one was open for 0% of the time, Pallas kernels for 11%

profile of v4, /device:TPU:4, one launch (start us, length us, event | category | flops | bytes accessed | tf_op | source)
XLA Modules:
  0.0 243.0 jit_solution(16081154446621140445)
XLA Ops:
  0.6 198.1 %shard_map.162 = (bf16[4,896,1024]{2,1,0:T(8,128)(2,1)}, bf16[4,896,512]{2,1,0:T(8,128)(2,1)}, bf16[4,896,512]{2,1,0:T(8,128)(2,1)}, bf16[256,1024]{1,0:T(8,128)...) custom-call(bf16[896,1024]{1,0:T(8,128)(2,1)} %wq.1, ...), custom_call_target="tpu_custom_call" | custom-call | tf_op jit(solution)/shard_map/pallas_call | solution.py:378
  198.8 1.3 collective-permute-start.1
  200.1 1.3 collective-permute-start.2
  201.4 0.7 collective-permute-start
  202.1 0.0 copy-start.9
  202.1 0.9 copy-done.9
  203.0 0.0 copy-start.10
  203.0 0.7 copy-done.10
  203.6 7.2 %shard_map.163 = (bf16[3,4,16,896]{3,2,1,0:T(8,128)(2,1)S(1)}, f32[4,4,1,224]{3,2,1,0:T(1,128)S(1)}) custom-call(bf16[4,16,896]{2,1,0:T(8,128)(2,1)S(1)} %copy-done.9, f32[4,1,224]{2,1,0:T(1,128)S(1)} %copy-done.10), custom_call_target="tpu_custom_call" | custom-call | flops 234881024 | bytes 7340032 | tf_op jit(solution)/shard_map/pallas_call | solution.py:413
  210.8 0.0 copy-start
  210.8 0.7 copy-done
  211.6 0.1 convert_reduce_fusion
  211.6 0.7 convert_element_type.7
  212.3 0.0 copy-start.1
  212.3 0.0 copy-start.4
  212.3 18.5 %shard_map.164 = (bf16[3584,1024]{1,0:T(8,128)(2,1)}, bf16[3584,512]{1,0:T(8,128)(2,1)}, bf16[3584,512]{1,0:T(8,128)(2,1)}, f32[1,1024]{1,0:T(1,128)}, f32[1,512]{1,0:T(1,128)}, /*index=5*/f32[1,512]{1,0:T(1,128)}) custom-call(bf16[4,896,1024]{2,1,0:T(8,128)(2,1)} %get-tuple-element.29.gq, bf16[4,896,512]{2,1,0:T(8,128)(2,1)} %get-tuple-element.30.gk, ...), custom_call_target="tpu_custom_call" | custom-call | flops 234881024 | bytes 29360128 | tf_op jit(solution)/shard_map/pallas_call | solution.py:445
  230.9 0.0 collective-permute-done.came
  230.9 0.0 copy-done.1
  230.9 0.0 copy-done.4
  230.9 0.0 copy-done.5
  230.9 0.0 copy-done.6
  230.9 0.0 copy-start.3
  230.9 0.0 copy-start.7
  230.9 0.1 shard_map.165
  231.0 0.0 collective-permute-done.1.came
  231.0 1.1 copy-done.3
  232.1 0.0 copy-done.7
  232.1 1.2 shard_map.166
  233.3 8.5 %collective-permute-done.2.came = bf16[896,512]{1,0:T(8,128)(2,1)S(1)} collective-permute-done((bf16[896,512]{1,0:T(8,128)(2,1)}, bf16[896,512]{1,0:T(8,128)(2,1)S(1)}, u32[]{:S(2)}, u32[]{:S(2)}) %collective-permute-start.2) | collective-permute-done | bytes 917536 | tf_op jit(solution)/shard_map/ppermute | solution.py:411
  241.8 0.0 copy-done.2
  241.8 0.0 copy-done.8
  241.8 1.2 shard_map.167
  (4 shorter events, 0.0 us)
Async XLA Ops:
  198.8 32.2 %collective-permute-start.1 = (bf16[896,512]{1,0:T(8,128)(2,1)}, bf16[896,512]{1,0:T(8,128)(2,1)S(1)}, u32[]{:S(2)}, u32[]{:S(2)}) collective-permute-start(bf16[896,512]{1,0:T(8,128)(2,1)} %get-tuple-element.33.tail), channel_id=1, source_target_pairs={{8,0},{16,24},{9,1},{17,25},{10,2},{18,26},{11,3},{19,27},{12,4},{... | collective-permute-start | bytes 2752520 | tf_op jit(solution)/shard_map/ppermute | solution.py:410
  200.1 41.7 %collective-permute-start.2 = (bf16[896,512]{1,0:T(8,128)(2,1)}, bf16[896,512]{1,0:T(8,128)(2,1)S(1)}, u32[]{:S(2)}, u32[]{:S(2)}) collective-permute-start(bf16[896,512]{1,0:T(8,128)(2,1)} %get-tuple-element.35.tail), channel_id=1, source_target_pairs={{8,0},{16,24},{9,1},{17,25},{10,2},{18,26},{11,3},{19,27},{12,4},{... | collective-permute-start | bytes 2752520 | tf_op jit(solution)/shard_map/ppermute | solution.py:411
  201.4 29.5 %collective-permute-start = (bf16[256,1024]{1,0:T(8,128)(2,1)}, bf16[256,1024]{1,0:T(8,128)(2,1)S(1)}, u32[]{:S(2)}, u32[]{:S(2)}) collective-permute-start(bf16[256,1024]{1,0:T(8,128)(2,1)} %get-tuple-element.24.tail), channel_id=1, source_target_pairs={{9,1},{17,25},{11,3},{19,27},{13,5},{21,29},{15,7},{23,31}} | collective-permute-start | bytes 1572872 | tf_op jit(solution)/shard_map/ppermute | solution.py:409
  202.1 0.9 copy-start.9
  203.0 0.7 copy-start.10
  210.8 0.7 copy-start
  212.3 18.6 %copy-start.1 = (bf16[3,4,16,896]{3,2,1,0:T(8,128)(2,1)S(1)}, bf16[3,4,16,896]{3,2,1,0:T(8,128)(2,1)}, u32[]{:S(2)}) copy-start(bf16[3,4,16,896]{3,2,1,0:T(8,128)(2,1)} %copy-done) | copy-start | bytes 1032196
  212.3 18.6 %copy-start.4 = (bf16[256,1024]{1,0:T(8,128)(2,1)S(1)}, bf16[256,1024]{1,0:T(8,128)(2,1)}, u32[]{:S(2)}) copy-start(bf16[256,1024]{1,0:T(8,128)(2,1)} %get-tuple-element.24.tail) | copy-start | bytes 1572868
  212.3 18.6 %copy-start.5 = (bf16[16,1024]{1,0:T(8,128)(2,1)S(1)}, bf16[16,1024]{1,0:T(8,128)(2,1)}, u32[]{:S(2)}) copy-start(bf16[16,1024]{1,0:T(8,128)(2,1)} %high.3) | copy-start | bytes 98308
  212.3 18.6 %copy-start.6 = (f32[1,2048]{1,0:T(1,128)S(1)}, f32[1,2048]{1,0:T(1,128)}, u32[]{:S(2)}) copy-start(f32[1,2048]{1,0:T(1,128)} %get-tuple-element.28.col_q.col_k.col_v.col) | copy-start | bytes 24580
  230.9 1.2 copy-start.3
  230.9 1.2 copy-start.7
  232.1 9.7 %copy-start.2 = (bf16[896,512]{1,0:T(8,128)(2,1)S(1)}, bf16[896,512]{1,0:T(8,128)(2,1)}, u32[]{:S(2)}) copy-start(bf16[896,512]{1,0:T(8,128)(2,1)} %get-tuple-element.35.tail) | copy-start | bytes 2752516
  232.1 9.7 %copy-start.8 = (bf16[16,512]{1,0:T(8,128)(2,1)S(1)}, bf16[16,512]{1,0:T(8,128)(2,1)}, u32[]{:S(2)}) copy-start(bf16[16,512]{1,0:T(8,128)(2,1)} %high.5) | copy-start | bytes 49156

commit v5 on v4

--- a/solution.py
+++ b/solution.py
@@ -21,8 +21,11 @@
     pieces = []
     for a, width in enumerate(widths):
         count = min(2 * (width // smallest), units)
-        cuts = [unit * (i * units // count) for i in range(count + 1)]
-        pieces += [(a, first, last - first) for first, last in zip(cuts, cuts[1:])]
+        cuts = [i * units // count for i in range(count + 1)]
+        if a == 2:
+            end = units - max(1, units // 7)
+            cuts = sorted({0, (end + 1) // 2, end, units})
+        pieces += [(a, unit * first, unit * (last - first)) for first, last in zip(cuts, cuts[1:])]
     return pieces
 
 
@@ -35,16 +38,15 @@
 
 
 def line_kernel(n, m, trials, wq, wk, wv, lq, lk, lv, hq, hk, hv, nt, ns,
-                gq, gk, gv, tail_q, tail_k, tail_v, glow, col_out, norm_out,
+                gq, gk, gv, tail_q, tail_k, tail_v, tail_w, glow, col_out, norm_out,
                 low_q, low_k, low_v, high_q, high_k, high_v, train, step_v, col_ref, norm_ref,
                 small_sem, result_sem,
-                own_q, own_k, own_v, vec, vec_own,
+                own_q, own_k, own_v, came, leaving, vec_own,
                 send_up, send_dn, recv_up, recv_dn,
                 low_send, low_recv, vec_send, vec_recv,
                 in_sem, out_sem, low_sem, above):
     z, x = lax.axis_index("fsdp"), lax.axis_index("width")
     weights, gathered, owns = (wq, wk, wv), (gq, gk, gv), (own_q, own_k, own_v)
-    asides = (tail_q, tail_k, tail_v)
     late = lax.axis_index("trial") == trials - 1
     lows, near_lows, near_highs = (lq, lk, lv), (low_q, low_k, low_v), (high_q, high_k, high_v)
     rows = wq.shape[0]
@@ -53,6 +55,12 @@
     count = len(pieces)
     spare = held_of(pieces)
 
+    def aside_of(c):
+        a, first, size = pieces[c]
+        if c == spare or c == count - 1:
+            return (tail_q if c == spare else tail_w).at[pl.ds(0, size)]
+        return (tail_k if a == 1 else tail_v).at[pl.ds(first, size)]
+
     loads = [pltpu.make_async_copy(w, o, in_sem.at[i]) for i, (w, o) in enumerate(zip(weights, owns))]
     smalls = [
         pltpu.make_async_copy(a, b, small_sem.at[i])
@@ -65,14 +73,8 @@
     def _():
         pl.semaphore_signal(barrier, inc=1, device_id_type=MESH, device_id={"fsdp": jnp.minimum(z + 1, n - 1)})
 
-    for copy in loads + smalls:
-        copy.start()
-
     def sent_block(hop, up):
         return jnp.clip(z - (hop - 1) if up else z + (hop - 1), 0, n - 1)
-
-    def came_block(hop, up):
-        return jnp.clip(z - hop if up else z + hop, 0, n - 1)
 
     def next_on(up):
         return jnp.clip(z + 1 if up else z - 1, 0, n - 1)
@@ -97,7 +99,7 @@
         landing = gathered[a].at[block, pl.ds(first, size)]
         source = weights[a].at[pl.ds(first, size)] if hop == 1 else landing
         if aside:
-            landing = asides[a].at[pl.ds(0 if c == spare else first, size)]
+            landing = aside_of(c)
         out, back = (send_up, recv_up) if up else (send_dn, recv_dn)
         return pltpu.make_async_remote_copy(
             src_ref=source, dst_ref=landing,
@@ -133,11 +135,10 @@
             send_sem=low_send.at[int(up), hop - 1], recv_sem=low_recv.at[int(up), hop - 1],
             device_id={"fsdp": next_on(up)}, device_id_type=MESH)
 
-    def vec_piece(hop, up):
-        block = sent_block(hop, up)
+    def message(up, first=False):
         return pltpu.make_async_remote_copy(
-            src_ref=vec_own if hop == 1 else vec.at[block], dst_ref=vec.at[block],
-            send_sem=vec_send.at[int(up), hop - 1], recv_sem=vec_recv.at[int(up), hop - 1],
+            src_ref=vec_own if first else leaving.at[int(up)], dst_ref=came.at[int(up)],
+            send_sem=vec_send.at[int(up)], recv_sem=vec_recv.at[int(up)],
             device_id={"fsdp": next_on(up)}, device_id_type=MESH)
 
     def carried(i):
@@ -167,6 +168,8 @@
         start_piece(1, c, True)
     start_low(True)
 
+    for copy in loads + smalls:
+        copy.start()
     for small in smalls:
         small.wait()
     for i in range(3):
@@ -179,6 +182,8 @@
     for store in stores:
         store.start()
     total = col_ref.shape[1]
+    slot = (vec_own.shape[1] - total) // n
+    vec_own[...] = jnp.zeros_like(vec_own)
     tile = 128 if rows % 128 == 0 else rows
     at = 0
     for low, high, own in zip(near_lows, near_highs, owns):
@@ -194,14 +199,16 @@
         vec_own[:, pl.ds(at, width)] = lax.fori_loop(0, rows // tile, step, jnp.zeros((1, width), F32))
         at += width
     gain = train[...] + step_v[...]
-    vec_own[:, pl.ds(total, share)] = gain
-    norm_ref[z] = gain
-    col_ref[...] = vec_own[:, pl.ds(0, total)]
-
-    for up in WAYS:
-        @pl.when(sends(1, up))
-        def _(up=up):
-            vec_piece(1, up).start()
+    for b in range(n):
+        vec_own[:, pl.ds(total + b * slot, share)] = jnp.where(z == b, gain, 0.0)
+
+    @pl.when(z == 0)
+    def _():
+        message(True, True).start()
+
+    @pl.when(z == n - 1)
+    def _():
+        message(False, True).start()
 
     for c in range(lead, count):
         for up in (False, True):
@@ -210,15 +217,23 @@
     results = [pltpu.make_async_copy(col_ref, col_out, result_sem.at[0]),
                pltpu.make_async_copy(norm_ref, norm_out, result_sem.at[1])]
 
+    def join(mine, other):
+        peak = jnp.maximum(mine[:, :total], other[:, :total])
+        return jnp.concatenate([peak, mine[:, total:] + other[:, total:]], axis=1)
+
     def small_turn(hop):
         for up in WAYS:
+            @pl.when((z == hop) if up else (z == n - 1 - hop))
+            def _(up=up):
+                message(up).wait_recv()
+
+                @pl.when((z < n - 1) if up else (z > 0))
+                def _():
+                    leaving[int(up)] = join(vec_own[...], came[int(up)])
+                    message(up).start()
+
             @pl.when(receives(hop, up))
             def _(up=up):
-                vec_piece(hop, up).wait_recv()
-                if hop < n - 1:
-                    @pl.when(sends(hop + 1, up))
-                    def _():
-                        vec_piece(hop + 1, up).start()
                 for i in range(3):
                     @pl.when(carried(i))
                     def _(i=i):
@@ -227,15 +242,20 @@
                             @pl.when(sends(hop + 1, up))
                             def _():
                                 low_piece(hop + 1, i, up).start()
-                block = came_block(hop, up)
-                came = vec[block]
-                col_ref[...] = jnp.maximum(col_ref[...], came[:, :total])
-                norm_ref[block] = came[:, total:total + share]
         if hop == n - 1:
+            col_ref[...] = vec_own[:, pl.ds(0, total)]
+            for b in range(n):
+                norm_ref[b] = vec_own[:, pl.ds(total + b * slot, share)]
+            for up in WAYS:
+                @pl.when((z > 0) if up else (z < n - 1))
+                def _(up=up):
+                    col_ref[...] = jnp.maximum(col_ref[...], came[int(up), :, pl.ds(0, total)])
+                    for b in range(n):
+                        norm_ref[b] += came[int(up), :, pl.ds(total + b * slot, share)]
             for result in results:
                 result.start()
 
-    turn = min(3, spare)
+    turn = min(1, spare)
     for hop in range(1, n):
         for c in range(count):
             if held(c) is True and hop == n - 1:
@@ -251,6 +271,15 @@
                 small_turn(hop)
     for copy in stores + results:
         copy.wait()
+
+    @pl.when(z < n - 1)
+    def _():
+        message(True).wait_send()
+
+    @pl.when(z > 0)
+    def _():
+        message(False).wait_send()
+
     for i in range(3):
         @pl.when(carried(i))
         def _(i=i):
@@ -259,7 +288,6 @@
         for up in WAYS:
             @pl.when(sends(hop, up))
             def _(hop=hop, up=up):
-                vec_piece(hop, up).wait_send()
                 for i in range(3):
                     @pl.when(carried(i))
                     def _(i=i):
@@ -370,12 +398,12 @@
     ck, cv = wk.shape[1], wv.shape[1]
     rank, share = hq.shape[0], nt.shape[0]
     total = cq + ck + cv
-    length = total + -(-share // 128) * 128
+    length = total + n * (-(-share // 128) * 128)
     pieces = pieces_of(rows, [cq, ck, cv])
     count, spare = len(pieces), held_of(pieces)
     hbm, vmem = pl.BlockSpec(memory_space=pl.ANY), pl.BlockSpec(memory_space=pltpu.VMEM)
     dma = pltpu.SemaphoreType.DMA
-    gq, gk, gv, tail_q, tail_k, tail_v, part, col, normz = pl.pallas_call(
+    gq, gk, gv, tail_q, tail_k, tail_v, tail_w, part, col, normz = pl.pallas_call(
         functools.partial(line_kernel, n, m, trials),
         out_shape=[
             jax.ShapeDtypeStruct((n, rows, cq), BF16),
@@ -383,22 +411,23 @@
             jax.ShapeDtypeStruct((n, rows, cv), BF16),
             jax.ShapeDtypeStruct((pieces[spare][2], cq), BF16),
             jax.ShapeDtypeStruct((rows, ck), BF16),
-            jax.ShapeDtypeStruct((rows, cv), BF16),
+            jax.ShapeDtypeStruct((rows - pieces[-1][2], cv), BF16),
+            jax.ShapeDtypeStruct((pieces[-1][2], cv), BF16),
             jax.ShapeDtypeStruct((n, rank, rows), BF16),
             jax.ShapeDtypeStruct((1, total), F32),
             jax.ShapeDtypeStruct((n, 1, share), F32),
         ],
         in_specs=[hbm] * 11,
-        out_specs=[hbm] * 9,
+        out_specs=[hbm] * 10,
         scratch_shapes=[
             pltpu.VMEM((rank, rows), BF16), pltpu.VMEM((rank, rows), BF16), pltpu.VMEM((rank, rows), BF16),
             pltpu.VMEM((rank, cq), BF16), pltpu.VMEM((rank, ck), BF16), pltpu.VMEM((rank, cv), BF16),
             pltpu.VMEM((1, share), F32), pltpu.VMEM((1, share), F32),
             pltpu.VMEM((1, total), F32), pltpu.VMEM((n, 1, share), F32), dma((8,)), dma((2,)),
             pltpu.VMEM((rows, cq), BF16), pltpu.VMEM((rows, ck), BF16), pltpu.VMEM((rows, cv), BF16),
-            pltpu.VMEM((n, 1, length), F32), pltpu.VMEM((1, length), F32),
+            pltpu.VMEM((2, 1, length), F32), pltpu.VMEM((2, 1, length), F32), pltpu.VMEM((1, length), F32),
             dma((n - 1, count)), dma((n - 1, count)), dma((n - 1, count)), dma((n - 1, count)),
-            dma((2, n - 1)), dma((2, n - 1)), dma((2, n - 1)), dma((2, n - 1)),
+            dma((2, n - 1)), dma((2, n - 1)), dma((2,)), dma((2,)),
             dma((3,)), dma((3,)), dma, pltpu.SemaphoreType.REGULAR,
         ],
         compiler_params=pltpu.CompilerParams(collective_id=0, has_side_effects=True),
@@ -409,6 +438,7 @@
     came_q = lax.ppermute(tail_q, ("fsdp", "trial"), lone)
     came_k = lax.ppermute(tail_k, "fsdp", ends)
     came_v = lax.ppermute(tail_v, "fsdp", ends)
+    came_w = lax.ppermute(tail_w, "fsdp", ends)
 
     glow, norm = pl.pallas_call(
         functools.partial(plane_kernel, m),
@@ -459,7 +489,7 @@
 
     def finish(i, came, tail, high, before, first, wanted):
         size, width = came.shape
-        step = 128 if rows % 128 == 0 else size
+        step = 128 if size % 128 == 0 else size
         start = starts[i]
         return pl.pallas_call(
             functools.partial(last_kernel, n, first, step, wanted),
@@ -480,7 +510,8 @@
 
     fq = finish(0, came_q, tail_q, hq, before_q, pieces[spare][1], trials - 1)
     fk = finish(1, came_k, tail_k, hk, before_k, 0, None)
-    fv = finish(2, came_v, tail_v, hv, before_v, 0, None)
+    most = finish(2, came_v, tail_v, hv, before_v, 0, None)
+    fv = finish(2, came_w, tail_w, hv, most, pieces[-1][1], None)
     return (fq, fk, fv, col_q[0], col_k[0], col_v[0], norm.reshape(-1).astype(BF16))
 
 

time: 244 us -> 244 us (level)
  transfers between devices with their start and end apart: 3 -> 4, of which waited for: 1 -> 2; matrix products, arithmetic and copies ran while one was open for 0% -> 0% of each run, Pallas kernels for 11% -> 11%
where the time goes in v5:
time: 244 us; the launch traced here: 243 us
  Pallas kernels  227 us (93%)
  waiting for transfers between devices  8.28 us (3%)
  starting transfers between devices  4.57 us (2%)
  local copies, waits for them, and re-layouts  3.07 us (1%)
    pallas_call x1, Pallas kernels, local(): pl.pallas_call(functools.partial(line_kernel, n, m, trials), out_shape=[j...  198 us
    pallas_call x1, Pallas kernels, local(): pl.pallas_call(functools.partial(merge_kernel, tile), grid=(halves, n), o...  18.5 us
    ppermute x1, waiting for transfers between devices, local(): came_v = lax.ppermute(tail_v, 'fsdp', ends)  8.06 us
    pallas_call x1, Pallas kernels, local(): pl.pallas_call(functools.partial(plane_kernel, m), out_shape=[jax.ShapeDt...  7.19 us
  transfers between devices with their start and end apart: 4, of which 2 were waited for; matrix products, arithmetic and copies ran while one was open for 0% of the time, Pallas kernels for 11%

profile of v5, /device:TPU:4, one launch (start us, length us, event | category | flops | bytes accessed | tf_op | source)
XLA Modules:
  0.0 243.5 jit_solution(12348701927304009726)
XLA Ops:
  0.6 197.7 %shard_map.162 = (bf16[4,896,1024]{2,1,0:T(8,128)(2,1)}, bf16[4,896,512]{2,1,0:T(8,128)(2,1)}, bf16[4,896,512]{2,1,0:T(8,128)(2,1)}, bf16[256,1024]{1,0:T(8,128)...) custom-call(bf16[896,1024]{1,0:T(8,128)(2,1)} %wq.1, ...), custom_call_target="tpu_custom_call" | custom-call | tf_op jit(solution)/shard_map/pallas_call | solution.py:406
  198.3 1.3 collective-permute-start.1
  199.6 1.3 collective-permute-start.3
  200.9 0.7 collective-permute-start
  201.6 1.3 collective-permute-start.2
  202.9 0.0 copy-start.10
  203.0 0.9 copy-done.10
  203.8 0.7 copy-done.11
  204.5 7.2 %shard_map.163 = (bf16[3,4,16,896]{3,2,1,0:T(8,128)(2,1)S(1)}, f32[4,4,1,224]{3,2,1,0:T(1,128)S(1)}) custom-call(bf16[4,16,896]{2,1,0:T(8,128)(2,1)S(1)} %copy-done.10, f32[4,1,224]{2,1,0:T(1,128)S(1)} %copy-done.11), custom_call_target="tpu_custom_call" | custom-call | flops 234881024 | bytes 7340032 | tf_op jit(solution)/shard_map/pallas_call | solution.py:443
  211.7 0.0 copy-start
  211.7 0.7 copy-done
  212.5 0.1 convert_reduce_fusion
  212.5 0.7 convert_element_type.7
  213.2 18.5 %shard_map.164 = (bf16[3584,1024]{1,0:T(8,128)(2,1)}, bf16[3584,512]{1,0:T(8,128)(2,1)}, bf16[3584,512]{1,0:T(8,128)(2,1)}, f32[1,1024]{1,0:T(1,128)}, f32[1,512]{1,0:T(1,128)}, /*index=5*/f32[1,512]{1,0:T(1,128)}) custom-call(bf16[4,896,1024]{2,1,0:T(8,128)(2,1)} %get-tuple-element.30.gq, bf16[4,896,512]{2,1,0:T(8,128)(2,1)} %get-tuple-element.31.gk, ...), custom_call_target="tpu_custom_call" | custom-call | flops 234881024 | bytes 29360128 | tf_op jit(solution)/shard_map/pallas_call | solution.py:475
  231.7 0.0 collective-permute-done.came
  231.8 0.0 copy-done.1
  231.8 0.0 copy-done.4
  231.8 0.0 copy-done.5
  231.8 0.0 copy-done.6
  231.8 0.0 copy-start.7
  231.8 0.1 shard_map.165
  231.9 8.1 %collective-permute-done.3.came = bf16[768,512]{1,0:T(8,128)(2,1)S(1)} collective-permute-done((bf16[768,512]{1,0:T(8,128)(2,1)}, bf16[768,512]{1,0:T(8,128)(2,1)S(1)}, u32[]{:S(2)}, u32[]{:S(2)}) %collective-permute-start.3) | collective-permute-done | bytes 786464 | tf_op jit(solution)/shard_map/ppermute | solution.py:440
  239.9 0.0 copy-done.7
  240.0 1.2 shard_map.167.before
  241.1 0.0 copy-start.8
  241.1 0.2 collective-permute-done.2.came
  241.4 0.0 copy-done.9
  241.4 0.9 shard_map.168
  242.2 0.0 collective-permute-done.1.came
  242.3 0.0 copy-done.2
  242.3 0.0 copy-done.8
  242.3 1.2 shard_map.166
  (9 shorter events, 0.0 us)
Async XLA Ops:
  198.3 43.9 %collective-permute-start.1 = (bf16[896,512]{1,0:T(8,128)(2,1)}, bf16[896,512]{1,0:T(8,128)(2,1)S(1)}, u32[]{:S(2)}, u32[]{:S(2)}) collective-permute-start(bf16[896,512]{1,0:T(8,128)(2,1)} %get-tuple-element.34.tail), channel_id=1, source_target_pairs={{8,0},{16,24},{9,1},{17,25},{10,2},{18,26},{11,3},{19,27},{12,4},{... | collective-permute-start | bytes 2752520 | tf_op jit(solution)/shard_map/ppermute | solution.py:439
  199.6 40.3 %collective-permute-start.3 = (bf16[768,512]{1,0:T(8,128)(2,1)}, bf16[768,512]{1,0:T(8,128)(2,1)S(1)}, u32[]{:S(2)}, u32[]{:S(2)}) collective-permute-start(bf16[768,512]{1,0:T(8,128)(2,1)} %get-tuple-element.37.tail), channel_id=1, source_target_pairs={{8,0},{16,24},{9,1},{17,25},{10,2},{18,26},{11,3},{19,27},{12,4},{... | collective-permute-start | bytes 2359304 | tf_op jit(solution)/shard_map/ppermute | solution.py:440
  200.9 30.8 %collective-permute-start = (bf16[256,1024]{1,0:T(8,128)(2,1)}, bf16[256,1024]{1,0:T(8,128)(2,1)S(1)}, u32[]{:S(2)}, u32[]{:S(2)}) collective-permute-start(bf16[256,1024]{1,0:T(8,128)(2,1)} %get-tuple-element.25.tail), channel_id=1, source_target_pairs={{9,1},{17,25},{11,3},{19,27},{13,5},{21,29},{15,7},{23,31}} | collective-permute-start | bytes 1572872 | tf_op jit(solution)/shard_map/ppermute | solution.py:438
  201.6 39.7 %collective-permute-start.2 = (bf16[128,512]{1,0:T(8,128)(2,1)}, bf16[128,512]{1,0:T(8,128)(2,1)S(1)}, u32[]{:S(2)}, u32[]{:S(2)}) collective-permute-start(bf16[128,512]{1,0:T(8,128)(2,1)} %get-tuple-element.36.tail), channel_id=1, source_target_pairs={{8,0},{16,24},{9,1},{17,25},{10,2},{18,26},{11,3},{19,27},{12,4},{... | collective-permute-start | bytes 393224 | tf_op jit(solution)/shard_map/ppermute | solution.py:441
  202.9 0.9 copy-start.10
  203.8 0.7 copy-start.11
  211.7 0.7 copy-start
  213.2 18.6 %copy-start.1 = (bf16[3,4,16,896]{3,2,1,0:T(8,128)(2,1)S(1)}, bf16[3,4,16,896]{3,2,1,0:T(8,128)(2,1)}, u32[]{:S(2)}) copy-start(bf16[3,4,16,896]{3,2,1,0:T(8,128)(2,1)} %copy-done) | copy-start | bytes 1032196
  213.2 18.6 %copy-start.4 = (bf16[256,1024]{1,0:T(8,128)(2,1)S(1)}, bf16[256,1024]{1,0:T(8,128)(2,1)}, u32[]{:S(2)}) copy-start(bf16[256,1024]{1,0:T(8,128)(2,1)} %get-tuple-element.25.tail) | copy-start | bytes 1572868
  213.2 18.6 %copy-start.5 = (f32[1,2048]{1,0:T(1,128)S(1)}, f32[1,2048]{1,0:T(1,128)}, u32[]{:S(2)}) copy-start(f32[1,2048]{1,0:T(1,128)} %get-tuple-element.29.col_q.col_k.col_v.col) | copy-start | bytes 24580
  213.2 18.6 %copy-start.6 = (bf16[16,1024]{1,0:T(8,128)(2,1)S(1)}, bf16[16,1024]{1,0:T(8,128)(2,1)}, u32[]{:S(2)}) copy-start(bf16[16,1024]{1,0:T(8,128)(2,1)} %high.4) | copy-start | bytes 98308
  231.8 8.2 %copy-start.3 = (bf16[768,512]{1,0:T(8,128)(2,1)S(1)}, bf16[768,512]{1,0:T(8,128)(2,1)}, u32[]{:S(2)}) copy-start(bf16[768,512]{1,0:T(8,128)(2,1)} %get-tuple-element.37.tail) | copy-start | bytes 2359300
  231.8 8.1 %copy-start.7 = (bf16[16,512]{1,0:T(8,128)(2,1)S(1)}, bf16[16,512]{1,0:T(8,128)(2,1)}, u32[]{:S(2)}) copy-start(bf16[16,512]{1,0:T(8,128)(2,1)} %high.7) | copy-start | bytes 49156
  240.0 1.4 copy-start.9
  241.1 1.2 copy-start.2
  241.1 1.2 copy-start.8

commit v6 on v5

--- a/solution.py
+++ b/solution.py
@@ -44,7 +44,7 @@
                 own_q, own_k, own_v, came, leaving, vec_own,
                 send_up, send_dn, recv_up, recv_dn,
                 low_send, low_recv, vec_send, vec_recv,
-                in_sem, out_sem, low_sem, above):
+                in_sem, out_sem, low_sem, inner):
     z, x = lax.axis_index("fsdp"), lax.axis_index("width")
     weights, gathered, owns = (wq, wk, wv), (gq, gk, gv), (own_q, own_k, own_v)
     late = lax.axis_index("trial") == trials - 1
@@ -68,10 +68,16 @@
     ]
 
     barrier = pltpu.get_barrier_semaphore()
-
-    @pl.when(z < n - 1)
-    def _():
-        pl.semaphore_signal(barrier, inc=1, device_id_type=MESH, device_id={"fsdp": jnp.minimum(z + 1, n - 1)})
+    middle = n // 2
+
+    def tell(semaphore, when, upward):
+        @pl.when(when)
+        def _():
+            pl.semaphore_signal(semaphore, inc=1, device_id_type=MESH, device_id={
+                "fsdp": jnp.minimum(z + 1, n - 1) if upward else jnp.maximum(z - 1, 0)})
+
+    tell(barrier, z < middle, True)
+    tell(barrier, z > middle, False)
 
     def sent_block(hop, up):
         return jnp.clip(z - (hop - 1) if up else z + (hop - 1), 0, n - 1)
@@ -144,10 +150,16 @@
     def carried(i):
         return x == carrier(i, m)
 
-    @pl.when(z > 0)
+    @pl.when((z > 0) & (z < n - 1) & (z != middle))
     def _():
         pl.semaphore_wait(barrier, 1)
-        pl.semaphore_signal(above, inc=1, device_id_type=MESH, device_id={"fsdp": jnp.maximum(z - 1, 0)})
+
+    @pl.when(z == middle)
+    def _():
+        pl.semaphore_wait(barrier, 2 if middle < n - 1 else 1)
+
+    tell(inner, (z > 0) & (z <= middle), False)
+    tell(inner, (z >= middle) & (z < n - 1), True)
 
     def start_low(up):
         for i in range(3):
@@ -156,17 +168,31 @@
                 low_piece(1, i, up).start()
 
     lead = min(3, count)
-    for c in range(lead):
-        start_piece(1, c, False)
-    start_low(False)
-
-    @pl.when(z < n - 1)
-    def _():
-        pl.semaphore_wait(above, 1)
-
-    for c in range(lead):
-        start_piece(1, c, True)
-    start_low(True)
+
+    def start_lead(up):
+        for c in range(lead):
+            start_piece(1, c, up)
+        start_low(up)
+
+    @pl.when(z <= middle)
+    def _():
+        start_lead(False)
+
+    @pl.when(z >= middle)
+    def _():
+        start_lead(True)
+
+    @pl.when(z != middle)
+    def _():
+        pl.semaphore_wait(inner, 1)
+
+    @pl.when(z < middle)
+    def _():
+        start_lead(True)
+
+    @pl.when(z > middle)
+    def _():
+        start_lead(False)
 
     for copy in loads + smalls:
         copy.start()

time: 244 us -> 244 us (level)
  no operation moved by 1% of the time
where the time goes in v6:
time: 244 us; the launch traced here: 243 us
  Pallas kernels  227 us (93%)
  waiting for transfers between devices  8.28 us (3%)
  starting transfers between devices  4.57 us (2%)
  local copies, waits for them, and re-layouts  3.08 us (1%)
    pallas_call x1, Pallas kernels, local(): pl.pallas_call(functools.partial(line_kernel, n, m, trials), out_shape=[j...  198 us
    pallas_call x1, Pallas kernels, local(): pl.pallas_call(functools.partial(merge_kernel, tile), grid=(halves, n), o...  18.5 us
    ppermute x1, waiting for transfers between devices, local(): came_v = lax.ppermute(tail_v, 'fsdp', ends)  8.06 us
    pallas_call x1, Pallas kernels, local(): pl.pallas_call(functools.partial(plane_kernel, m), out_shape=[jax.ShapeDt...  7.19 us
  transfers between devices with their start and end apart: 4, of which 2 were waited for; matrix products, arithmetic and copies ran while one was open for 0% of the time, Pallas kernels for 11%

profile of v6, /device:TPU:4, one launch (start us, length us, event | category | flops | bytes accessed | tf_op | source)
XLA Modules:
  0.0 243.5 jit_solution(6473880682349494983)
XLA Ops:
  0.6 197.7 %shard_map.162 = (bf16[4,896,1024]{2,1,0:T(8,128)(2,1)}, bf16[4,896,512]{2,1,0:T(8,128)(2,1)}, bf16[4,896,512]{2,1,0:T(8,128)(2,1)}, bf16[256,1024]{1,0:T(8,128)...) custom-call(bf16[896,1024]{1,0:T(8,128)(2,1)} %wq.1, ...), custom_call_target="tpu_custom_call" | custom-call | tf_op jit(solution)/shard_map/pallas_call | solution.py:432
  198.3 1.3 collective-permute-start.1
  199.6 1.3 collective-permute-start.3
  200.9 0.7 collective-permute-start
  201.7 1.3 collective-permute-start.2
  202.9 0.0 copy-start.10
  203.0 0.9 copy-done.10
  203.9 0.7 copy-done.11
  204.5 7.2 %shard_map.163 = (bf16[3,4,16,896]{3,2,1,0:T(8,128)(2,1)S(1)}, f32[4,4,1,224]{3,2,1,0:T(1,128)S(1)}) custom-call(bf16[4,16,896]{2,1,0:T(8,128)(2,1)S(1)} %copy-done.10, f32[4,1,224]{2,1,0:T(1,128)S(1)} %copy-done.11), custom_call_target="tpu_custom_call" | custom-call | flops 234881024 | bytes 7340032 | tf_op jit(solution)/shard_map/pallas_call | solution.py:469
  211.7 0.0 copy-start
  211.7 0.7 copy-done
  212.5 0.1 convert_reduce_fusion
  212.5 0.7 convert_element_type.7
  213.2 18.5 %shard_map.164 = (bf16[3584,1024]{1,0:T(8,128)(2,1)}, bf16[3584,512]{1,0:T(8,128)(2,1)}, bf16[3584,512]{1,0:T(8,128)(2,1)}, f32[1,1024]{1,0:T(1,128)}, f32[1,512]{1,0:T(1,128)}, /*index=5*/f32[1,512]{1,0:T(1,128)}) custom-call(bf16[4,896,1024]{2,1,0:T(8,128)(2,1)} %get-tuple-element.30.gq, bf16[4,896,512]{2,1,0:T(8,128)(2,1)} %get-tuple-element.31.gk, ...), custom_call_target="tpu_custom_call" | custom-call | flops 234881024 | bytes 29360128 | tf_op jit(solution)/shard_map/pallas_call | solution.py:501
  231.7 0.0 collective-permute-done.came
  231.8 0.0 copy-done.1
  231.8 0.0 copy-done.4
  231.8 0.0 copy-done.5
  231.8 0.0 copy-done.6
  231.8 0.0 copy-start.3
  231.8 0.0 copy-start.7
  231.8 0.1 shard_map.165
  231.9 8.1 %collective-permute-done.3.came = bf16[768,512]{1,0:T(8,128)(2,1)S(1)} collective-permute-done((bf16[768,512]{1,0:T(8,128)(2,1)}, bf16[768,512]{1,0:T(8,128)(2,1)S(1)}, u32[]{:S(2)}, u32[]{:S(2)}) %collective-permute-start.3) | collective-permute-done | bytes 786464 | tf_op jit(solution)/shard_map/ppermute | solution.py:466
  239.9 0.0 copy-done.7
  240.0 1.2 shard_map.167.before
  241.1 0.0 copy-start.8
  241.1 0.2 collective-permute-done.2.came
  241.3 0.0 copy-done.9
  241.4 0.9 shard_map.168
  242.2 0.0 collective-permute-done.1.came
  242.2 0.1 copy-done.2
  242.3 1.2 shard_map.166
  (9 shorter events, 0.0 us)
Async XLA Ops:
  198.3 43.9 %collective-permute-start.1 = (bf16[896,512]{1,0:T(8,128)(2,1)}, bf16[896,512]{1,0:T(8,128)(2,1)S(1)}, u32[]{:S(2)}, u32[]{:S(2)}) collective-permute-start(bf16[896,512]{1,0:T(8,128)(2,1)} %get-tuple-element.34.tail), channel_id=1, source_target_pairs={{8,0},{16,24},{9,1},{17,25},{10,2},{18,26},{11,3},{19,27},{12,4},{... | collective-permute-start | bytes 2752520 | tf_op jit(solution)/shard_map/ppermute | solution.py:465
  199.6 40.3 %collective-permute-start.3 = (bf16[768,512]{1,0:T(8,128)(2,1)}, bf16[768,512]{1,0:T(8,128)(2,1)S(1)}, u32[]{:S(2)}, u32[]{:S(2)}) collective-permute-start(bf16[768,512]{1,0:T(8,128)(2,1)} %get-tuple-element.37.tail), channel_id=1, source_target_pairs={{8,0},{16,24},{9,1},{17,25},{10,2},{18,26},{11,3},{19,27},{12,4},{... | collective-permute-start | bytes 2359304 | tf_op jit(solution)/shard_map/ppermute | solution.py:466
  200.9 30.8 %collective-permute-start = (bf16[256,1024]{1,0:T(8,128)(2,1)}, bf16[256,1024]{1,0:T(8,128)(2,1)S(1)}, u32[]{:S(2)}, u32[]{:S(2)}) collective-permute-start(bf16[256,1024]{1,0:T(8,128)(2,1)} %get-tuple-element.25.tail), channel_id=1, source_target_pairs={{9,1},{17,25},{11,3},{19,27},{13,5},{21,29},{15,7},{23,31}} | collective-permute-start | bytes 1572872 | tf_op jit(solution)/shard_map/ppermute | solution.py:464
  201.7 39.7 %collective-permute-start.2 = (bf16[128,512]{1,0:T(8,128)(2,1)}, bf16[128,512]{1,0:T(8,128)(2,1)S(1)}, u32[]{:S(2)}, u32[]{:S(2)}) collective-permute-start(bf16[128,512]{1,0:T(8,128)(2,1)} %get-tuple-element.36.tail), channel_id=1, source_target_pairs={{8,0},{16,24},{9,1},{17,25},{10,2},{18,26},{11,3},{19,27},{12,4},{... | collective-permute-start | bytes 393224 | tf_op jit(solution)/shard_map/ppermute | solution.py:467
  202.9 0.9 copy-start.10
  203.8 0.7 copy-start.11
  211.7 0.7 copy-start
  213.2 18.6 %copy-start.1 = (bf16[3,4,16,896]{3,2,1,0:T(8,128)(2,1)S(1)}, bf16[3,4,16,896]{3,2,1,0:T(8,128)(2,1)}, u32[]{:S(2)}) copy-start(bf16[3,4,16,896]{3,2,1,0:T(8,128)(2,1)} %copy-done) | copy-start | bytes 1032196
  213.2 18.6 %copy-start.4 = (bf16[256,1024]{1,0:T(8,128)(2,1)S(1)}, bf16[256,1024]{1,0:T(8,128)(2,1)}, u32[]{:S(2)}) copy-start(bf16[256,1024]{1,0:T(8,128)(2,1)} %get-tuple-element.25.tail) | copy-start | bytes 1572868
  213.2 18.6 %copy-start.5 = (f32[1,2048]{1,0:T(1,128)S(1)}, f32[1,2048]{1,0:T(1,128)}, u32[]{:S(2)}) copy-start(f32[1,2048]{1,0:T(1,128)} %get-tuple-element.29.col_q.col_k.col_v.col) | copy-start | bytes 24580
  213.2 18.6 %copy-start.6 = (bf16[16,1024]{1,0:T(8,128)(2,1)S(1)}, bf16[16,1024]{1,0:T(8,128)(2,1)}, u32[]{:S(2)}) copy-start(bf16[16,1024]{1,0:T(8,128)(2,1)} %high.4) | copy-start | bytes 98308
  231.8 8.2 %copy-start.3 = (bf16[768,512]{1,0:T(8,128)(2,1)S(1)}, bf16[768,512]{1,0:T(8,128)(2,1)}, u32[]{:S(2)}) copy-start(bf16[768,512]{1,0:T(8,128)(2,1)} %get-tuple-element.37.tail) | copy-start | bytes 2359300
  231.8 8.1 %copy-start.7 = (bf16[16,512]{1,0:T(8,128)(2,1)S(1)}, bf16[16,512]{1,0:T(8,128)(2,1)}, u32[]{:S(2)}) copy-start(bf16[16,512]{1,0:T(8,128)(2,1)} %high.7) | copy-start | bytes 49156
  240.0 1.4 copy-start.9
  241.1 1.2 copy-start.2
  241.1 1.2 copy-start.8

commit v7 on v6

--- a/solution.py
+++ b/solution.py
@@ -158,9 +158,6 @@
     def _():
         pl.semaphore_wait(barrier, 2 if middle < n - 1 else 1)
 
-    tell(inner, (z > 0) & (z <= middle), False)
-    tell(inner, (z >= middle) & (z < n - 1), True)
-
     def start_low(up):
         for i in range(3):
             @pl.when(carried(i) & sends(1, up))
@@ -174,13 +171,16 @@
             start_piece(1, c, up)
         start_low(up)
 
+    @pl.when(z >= middle)
+    def _():
+        start_lead(True)
+
     @pl.when(z <= middle)
     def _():
         start_lead(False)
 
-    @pl.when(z >= middle)
-    def _():
-        start_lead(True)
+    tell(inner, (z > 0) & (z <= middle), False)
+    tell(inner, (z >= middle) & (z < n - 1), True)
 
     @pl.when(z != middle)
     def _():
@@ -417,6 +417,38 @@
         @pl.when(here)
         def _(source=source, low=low, block=block):
             write(source, low, block)
+
+
+def ready_kernel(first, low_first, low_last, high, col, plus, scale):
+    z = lax.axis_index("fsdp")
+    size = plus.shape[0]
+    scale[...] = 1.0 / col[...]
+
+    def fill(low):
+        plus[...] = mix_rate * lax.dot_general(
+            low[0, 0, :, pl.ds(first, size)], high[...], (((0,), (0,)), ((), ())), preferred_element_type=F32)
+
+    @pl.when(z < 2)
+    def _():
+        fill(low_last)
+
+    @pl.when(z >= 2)
+    def _():
+        fill(low_first)
+
+
+def close_kernel(n, first, came, tail, plus, scale, before, final, out_ref, out_sem):
+    z = lax.axis_index("fsdp")
+    size = came.shape[0]
+    rows = final.shape[0] // n
+
+    for at, source, block in ((0, came, n - 1), (1, tail, n - 1), (n - 2, tail, 0), (n - 1, came, 0)):
+        @pl.when(z == at)
+        def _(source=source, block=block):
+            out_ref[...] = ((source[...].astype(F32) + plus[...]) * scale[...]).astype(BF16)
+            store = pltpu.make_async_copy(out_ref, final.at[pl.ds(block * rows + first, size)], out_sem)
+            store.start()
+            store.wait()
 
 
 def local(n, m, trials, wq, lq, hq, wk, lk, hk, wv, lv, hv, nt, ns):
@@ -537,7 +569,30 @@
     fq = finish(0, came_q, tail_q, hq, before_q, pieces[spare][1], trials - 1)
     fk = finish(1, came_k, tail_k, hk, before_k, 0, None)
     most = finish(2, came_v, tail_v, hv, before_v, 0, None)
-    fv = finish(2, came_w, tail_w, hv, most, pieces[-1][1], None)
+    first, size = pieces[-1][1], pieces[-1][2]
+    plus, scale = pl.pallas_call(
+        functools.partial(ready_kernel, first),
+        grid=(1,),
+        out_shape=[jax.ShapeDtypeStruct((size, cv), F32), jax.ShapeDtypeStruct((1, cv), F32)],
+        in_specs=[pl.BlockSpec((1, 1, rank, rows), lambda t: (2, 0, 0, 0)),
+                  pl.BlockSpec((1, 1, rank, rows), lambda t: (2, n - 1, 0, 0)),
+                  vmem, pl.BlockSpec((1, cv), lambda t: (0, starts[2] // cv))],
+        out_specs=[vmem] * 2,
+        compiler_params=pltpu.CompilerParams(vmem_limit_bytes=12 * 2**20),
+        cost_estimate=pl.CostEstimate(
+            flops=2 * size * cv * rank, bytes_accessed=4 * size * cv, transcendentals=0),
+    )(glow, glow, hv, col)
+    fv = pl.pallas_call(
+        functools.partial(close_kernel, n, first),
+        out_shape=jax.ShapeDtypeStruct((n * rows, cv), BF16),
+        in_specs=[vmem] * 4 + [hbm],
+        out_specs=hbm,
+        scratch_shapes=[pltpu.VMEM((size, cv), BF16), dma],
+        input_output_aliases={4: 0},
+        compiler_params=pltpu.CompilerParams(vmem_limit_bytes=12 * 2**20),
+        cost_estimate=pl.CostEstimate(
+            flops=2 * size * cv, bytes_accessed=4 * size * cv, transcendentals=0),
+    )(came_w, tail_w, plus, scale, most)
     return (fq, fk, fv, col_q[0], col_k[0], col_v[0], norm.reshape(-1).astype(BF16))
 
 

time: 244 us -> 244 us (level)
  no operation moved by 1% of the time
where the time goes in v7:
time: 244 us
  Pallas kernels  227 us (93%)
  waiting for transfers between devices  7.16 us (3%)
  starting transfers between devices  4.57 us (2%)
  local copies, waits for them, and re-layouts  4.48 us (2%)
    pallas_call x1, Pallas kernels, local(): pl.pallas_call(functools.partial(line_kernel, n, m, trials), out_shape=[j...  198 us
    pallas_call x1, Pallas kernels, local(): pl.pallas_call(functools.partial(merge_kernel, tile), grid=(halves, n), o...  18.5 us
    pallas_call x1, Pallas kernels, local(): pl.pallas_call(functools.partial(plane_kernel, m), out_shape=[jax.ShapeDt...  7.19 us
    ppermute x1, waiting for transfers between devices, local(): came_v = lax.ppermute(tail_v, 'fsdp', ends)  6.94 us
  transfers between devices with their start and end apart: 4, of which 2 were waited for; matrix products, arithmetic and copies ran while one was open for 0% of the time, Pallas kernels for 11%

profile of v7, /device:TPU:4, one launch (start us, length us, event | category | flops | bytes accessed | tf_op | source)
XLA Modules:
  0.0 243.8 jit_solution(5837139992012625822)
XLA Ops:
  0.6 0.0 copy-start.9
  0.6 197.7 %shard_map.162 = (bf16[4,896,1024]{2,1,0:T(8,128)(2,1)}, bf16[4,896,512]{2,1,0:T(8,128)(2,1)}, bf16[4,896,512]{2,1,0:T(8,128)(2,1)}, bf16[256,1024]{1,0:T(8,128)...) custom-call(bf16[896,1024]{1,0:T(8,128)(2,1)} %wq.1, ...), custom_call_target="tpu_custom_call" | custom-call | tf_op jit(solution)/shard_map/pallas_call | solution.py:464
  198.4 1.3 collective-permute-start.1
  199.7 1.3 collective-permute-start.3
  201.0 0.7 collective-permute-start
  201.7 1.3 collective-permute-start.2
  203.0 0.0 copy-start.13
  203.0 0.9 copy-done.13
  203.9 0.7 copy-done.14
  204.5 7.2 %shard_map.163 = (bf16[3,4,16,896]{3,2,1,0:T(8,128)(2,1)S(1)}, f32[4,4,1,224]{3,2,1,0:T(1,128)S(1)}) custom-call(bf16[4,16,896]{2,1,0:T(8,128)(2,1)S(1)} %copy-done.13, f32[4,1,224]{2,1,0:T(1,128)S(1)} %copy-done.14), custom_call_target="tpu_custom_call" | custom-call | flops 234881024 | bytes 7340032 | tf_op jit(solution)/shard_map/pallas_call | solution.py:501
  211.7 0.0 copy-start
  211.7 0.1 convert_reduce_fusion
  211.8 0.7 convert_element_type.7
  212.5 0.0 copy-done.9
  212.5 0.7 copy-done.6
  213.2 0.2 shard_map.167
  213.4 0.0 copy-done
  213.4 0.0 copy-start.5
  213.4 0.0 copy-start.7
  213.4 0.0 copy-start.8
  213.5 18.5 %shard_map.164 = (bf16[3584,1024]{1,0:T(8,128)(2,1)}, bf16[3584,512]{1,0:T(8,128)(2,1)}, bf16[3584,512]{1,0:T(8,128)(2,1)}, f32[1,1024]{1,0:T(1,128)}, f32[1,512]{1,0:T(1,128)}, /*index=5*/f32[1,512]{1,0:T(1,128)}) custom-call(bf16[4,896,1024]{2,1,0:T(8,128)(2,1)} %get-tuple-element.32.gq, bf16[4,896,512]{2,1,0:T(8,128)(2,1)} %get-tuple-element.33.gk, ...), custom_call_target="tpu_custom_call" | custom-call | flops 234881024 | bytes 29360128 | tf_op jit(solution)/shard_map/pallas_call | solution.py:533
  232.0 0.0 collective-permute-done.came
  232.0 0.0 copy-done.5
  232.0 0.0 copy-done.7
  232.0 1.0 copy-done.1
  233.0 6.9 %collective-permute-done.3.came = bf16[768,512]{1,0:T(8,128)(2,1)S(1)} collective-permute-done((bf16[768,512]{1,0:T(8,128)(2,1)}, bf16[768,512]{1,0:T(8,128)(2,1)S(1)}, u32[]{:S(2)}, u32[]{:S(2)}) %collective-permute-start.3) | collective-permute-done | bytes 786464 | tf_op jit(solution)/shard_map/ppermute | solution.py:498
  240.0 1.2 shard_map.168.before
  241.1 0.2 collective-permute-done.2.came
  241.4 0.7 shard_map.169
  242.1 0.0 collective-permute-done.1.came
  242.1 0.5 copy-done.3
  242.6 1.2 shard_map.166
  (16 shorter events, 0.0 us)
Async XLA Ops:
  0.6 211.9 %copy-start.9 = (bf16[16,512]{1,0:T(8,128)(2,1)S(1)}, bf16[16,512]{1,0:T(8,128)(2,1)}, u32[]{:S(2)}) copy-start(bf16[16,512]{1,0:T(8,128)(2,1)} %high.7) | copy-start | bytes 49156
  198.4 43.7 %collective-permute-start.1 = (bf16[896,512]{1,0:T(8,128)(2,1)}, bf16[896,512]{1,0:T(8,128)(2,1)S(1)}, u32[]{:S(2)}, u32[]{:S(2)}) collective-permute-start(bf16[896,512]{1,0:T(8,128)(2,1)} %get-tuple-element.36.tail), channel_id=1, source_target_pairs={{8,0},{16,24},{9,1},{17,25},{10,2},{18,26},{11,3},{19,27},{12,4},{... | collective-permute-start | bytes 2752520 | tf_op jit(solution)/shard_map/ppermute | solution.py:497
  199.7 40.3 %collective-permute-start.3 = (bf16[768,512]{1,0:T(8,128)(2,1)}, bf16[768,512]{1,0:T(8,128)(2,1)S(1)}, u32[]{:S(2)}, u32[]{:S(2)}) collective-permute-start(bf16[768,512]{1,0:T(8,128)(2,1)} %get-tuple-element.41.tail), channel_id=1, source_target_pairs={{8,0},{16,24},{9,1},{17,25},{10,2},{18,26},{11,3},{19,27},{12,4},{... | collective-permute-start | bytes 2359304 | tf_op jit(solution)/shard_map/ppermute | solution.py:498
  201.0 31.0 %collective-permute-start = (bf16[256,1024]{1,0:T(8,128)(2,1)}, bf16[256,1024]{1,0:T(8,128)(2,1)S(1)}, u32[]{:S(2)}, u32[]{:S(2)}) collective-permute-start(bf16[256,1024]{1,0:T(8,128)(2,1)} %get-tuple-element.27.tail), channel_id=1, source_target_pairs={{9,1},{17,25},{11,3},{19,27},{13,5},{21,29},{15,7},{23,31}} | collective-permute-start | bytes 1572872 | tf_op jit(solution)/shard_map/ppermute | solution.py:496
  201.7 39.7 %collective-permute-start.2 = (bf16[128,512]{1,0:T(8,128)(2,1)}, bf16[128,512]{1,0:T(8,128)(2,1)S(1)}, u32[]{:S(2)}, u32[]{:S(2)}) collective-permute-start(bf16[128,512]{1,0:T(8,128)(2,1)} %get-tuple-element.38.tail), channel_id=1, source_target_pairs={{8,0},{16,24},{9,1},{17,25},{10,2},{18,26},{11,3},{19,27},{12,4},{... | collective-permute-start | bytes 393224 | tf_op jit(solution)/shard_map/ppermute | solution.py:499
  203.0 0.9 copy-start.13
  203.9 0.7 copy-start.14
  211.7 1.7 copy-start
  212.5 0.7 copy-start.6
  213.4 18.6 %copy-start.5 = (bf16[256,1024]{1,0:T(8,128)(2,1)S(1)}, bf16[256,1024]{1,0:T(8,128)(2,1)}, u32[]{:S(2)}) copy-start(bf16[256,1024]{1,0:T(8,128)(2,1)} %get-tuple-element.27.tail) | copy-start | bytes 1572868
  213.4 18.6 %copy-start.7 = (f32[1,2048]{1,0:T(1,128)S(1)}, f32[1,2048]{1,0:T(1,128)}, u32[]{:S(2)}) copy-start(f32[1,2048]{1,0:T(1,128)} %get-tuple-element.31.col_q.col_k.col_v.col) | copy-start | bytes 24580
  213.4 18.6 %copy-start.8 = (bf16[16,1024]{1,0:T(8,128)(2,1)S(1)}, bf16[16,1024]{1,0:T(8,128)(2,1)}, u32[]{:S(2)}) copy-start(bf16[16,1024]{1,0:T(8,128)(2,1)} %high.4) | copy-start | bytes 98308
  232.0 1.0 copy-start.1
  233.0 7.0 %copy-start.2 = (bf16[3,4,16,896]{3,2,1,0:T(8,128)(2,1)S(1)}, bf16[3,4,16,896]{3,2,1,0:T(8,128)(2,1)}, u32[]{:S(2)}) copy-start(bf16[3,4,16,896]{3,2,1,0:T(8,128)(2,1)} %copy-done) | copy-start | bytes 1032196
  233.0 7.0 %copy-start.4 = (bf16[768,512]{1,0:T(8,128)(2,1)S(1)}, bf16[768,512]{1,0:T(8,128)(2,1)}, u32[]{:S(2)}) copy-start(bf16[768,512]{1,0:T(8,128)(2,1)} %get-tuple-element.41.tail) | copy-start | bytes 2359300
  233.0 7.0 %copy-start.10 = (bf16[16,512]{1,0:T(8,128)(2,1)S(1)}, bf16[16,512]{1,0:T(8,128)(2,1)}, u32[]{:S(2)}) copy-start(bf16[16,512]{1,0:T(8,128)(2,1)} %high.7) | copy-start | bytes 49156
  240.0 1.4 copy-start.12
  241.4 1.2 copy-start.3
  241.4 1.2 copy-start.11
